TPU v7x, 512 devices: a whole 4x8x8 slice. The times are simulated.
512 devices in a mesh: seq: 128 (over y, z, core), head: 4 (over x).
Axes of the slice: x: 4, y: 8, z: 8, core: 2. Of those that a mesh axis runs over, the one named last changes fastest.
Arguments:
- queries: bfloat16 [16384, 1536], P('seq', 'head'), may hold values from -400 to 400
- latent: bfloat16 [16384, 320], P(('seq', 'head')), may hold values from -6 to 6
- w_kv_up: bfloat16 [256, 2048], P(None, 'head'), may hold values from -0.375 to 0.375
Outputs:
- attended: bfloat16 [16384, 1024], P('seq', 'head')
All inputs are finite; a program needn't handle non-finite values.
Results may differ from a plain program's by a relative error of at most 0.004.
Values may be sent and summed in bfloat16 or wider, within the bound.
No kernel may reach another device: no remote copies, remote signals or barrier semaphores. Data moves between devices by JAX's collectives and lax.ppermute only.
A program may use at most 64 MiB of HBM per device.

v0:
```python
import math

import jax
import jax.numpy as jnp
from jax import lax
from jax.experimental import pallas as pl
from jax.experimental.pallas import tpu as pltpu
from jax.sharding import Mesh
from jax.sharding import PartitionSpec as P

D_LATENT = 256
ROPE = 64
NOPE = 128
VDIM = 128
MASKED = -1e30
LOG2_SCALE = math.log2(math.e) * (NOPE + ROPE) ** -0.5


YS, ZS, CS, XS = 8, 8, 2, 4
GROUP = 128
KEYS = 32
UNIT = 2 * GROUP
CHUNK = ZS * KEYS
PACKED = KEYS * (D_LATENT + ROPE) // 128
VMEM_LIMIT = 20 * 2**20
OUT_ROWS = 2 * VDIM + 16
NT = (((1,), (1,)), ((), ()))
f32, bf16 = jnp.float32, jnp.bfloat16


def split(value):
    high = value.astype(bf16)
    return high, (value - high.astype(f32)).astype(bf16)


def query_kernel(*refs):
    qcat_ref, values_ref = refs[XS:]
    for k in range(XS):
        qw_ref = refs[k]
        rope = qw_ref[2 * GROUP : 3 * GROUP].astype(f32).T * LOG2_SCALE
        for h in range(2):
            nope = qw_ref[h * GROUP : (h + 1) * GROUP]
            start = 3 * GROUP + h * 2 * D_LATENT
            w_key = qw_ref[start : start + D_LATENT]
            side = lax.dot_general(w_key, nope, NT, preferred_element_type=f32) * LOG2_SCALE
            values_ref[2 * k + h] = qw_ref[start + D_LATENT : start + 2 * D_LATENT].T
            cols = pl.ds((2 * k + h) * GROUP, GROUP)
            high, low = split(side)
            qcat_ref[0:256, cols] = high
            qcat_ref[256:512, cols] = low
            high, low = split(rope[h * ROPE : (h + 1) * ROPE])
            none = jnp.zeros((ROPE, GROUP), bf16)
            qcat_ref[512:768, cols] = jnp.concatenate([high, none, low, none], axis=0)


def one_chunk(kv_ref, row, masks, qcat_ref, m_ref, l_ref, acc_ref):
    block = kv_ref[pl.ds(row * ZS, ZS)]
    latent = jnp.concatenate(
        [block[:, 0:KEYS].reshape(CHUNK, 128), block[:, KEYS : 2 * KEYS].reshape(CHUNK, 128)], axis=1
    )
    packed = block[:, 2 * KEYS :].astype(f32)
    other = pltpu.roll(packed.reshape(CHUNK // 2, 128), 64, 1).reshape(packed.shape)
    rope = jnp.concatenate([packed, other], axis=1).astype(bf16).reshape(CHUNK, 128)
    keys = jnp.concatenate([latent, latent, rope, rope], axis=1)
    turned = latent.T
    units = [pl.ds(u * UNIT, UNIT) for u in range(XS)]
    scores = [jnp.dot(keys, qcat_ref[:, cols], preferred_element_type=f32) for cols in units]
    for u, cols in enumerate(units):
        s = scores[u]
        if masks is not None:
            s = jnp.where(masks, s, MASKED)
        m_old = m_ref[:, cols]
        m_new = jnp.maximum(m_old, jnp.max(s, axis=0, keepdims=True))
        factor = jnp.exp2(m_old - m_new)
        weights = jnp.exp2(s - m_new)
        if masks is not None:
            weights = jnp.where(masks, weights, 0.0)
        l_ref[:, cols] = l_ref[:, cols] * factor + jnp.sum(weights, axis=0, keepdims=True)
        m_ref[:, cols] = m_new
        update = jnp.dot(turned, weights.astype(bf16), preferred_element_type=f32)
        acc_ref[:, cols] = acc_ref[:, cols] * factor + update


def attend(kv_ref, from_other, qcat_ref, m_ref, l_ref, acc_ref):
    y, z, c, x = (lax.axis_index(a) for a in ("y", "z", "c", "x"))
    key_core = 1 - c if from_other else c
    key = lax.broadcasted_iota(jnp.int32, (CHUNK, UNIT), 0)
    row = lax.broadcasted_iota(jnp.int32, (CHUNK, UNIT), 1) % GROUP
    query_pos = (z * 2 + c) * GROUP + row
    key_pos = ((key // KEYS) * 2 + key_core) * GROUP + x * KEYS + key % KEYS
    refs = (qcat_ref, m_ref, l_ref, acc_ref)
    one_chunk(kv_ref, y, key_pos <= query_pos, *refs)
    lax.fori_loop(0, y, lambda i, _: one_chunk(kv_ref, i, None, *refs), None)


def first_kernel(kv_ref, qcat_ref, m_ref, l_ref, acc_ref):
    m_ref[...] = jnp.full(m_ref.shape, MASKED, f32)
    l_ref[...] = jnp.zeros(l_ref.shape, f32)
    acc_ref[...] = jnp.zeros(acc_ref.shape, f32)
    attend(kv_ref, False, qcat_ref, m_ref, l_ref, acc_ref)


def thirds(value):
    high, _ = split(value)
    middle, low = split(value - high.astype(f32))
    return [high, middle, low]


def second_kernel(values_ref, kv_ref, qcat_ref, m_in, l_in, acc_in, out_ref, m_ref, l_ref, acc_ref):
    m_ref[...] = m_in[...]
    l_ref[...] = l_in[...]
    acc_ref[...] = acc_in[...]
    attend(kv_ref, True, qcat_ref, m_ref, l_ref, acc_ref)
    x = lax.axis_index("x")
    for k in range(XS):
        owner = lax.rem(x + XS - k, XS)
        stats = []
        for h in range(2):
            cols = pl.ds((2 * k + h) * GROUP, GROUP)
            w_value = values_ref[2 * k + h]
            high, low = split(acc_ref[:, cols])
            part = jnp.dot(w_value, high, preferred_element_type=f32)
            part = part + jnp.dot(w_value, low, preferred_element_type=f32)
            out_ref[owner, h * VDIM : (h + 1) * VDIM] = part.astype(bf16)
            stats += thirds(m_ref[:, cols]) + thirds(l_ref[:, cols])
        stats.append(jnp.zeros((4, GROUP), bf16))
        out_ref[owner, 2 * VDIM :] = jnp.concatenate([t.astype(f32) for t in stats], axis=0).astype(bf16)


def combine_kernel(parts_ref, out_ref):
    stats = [parts_ref[k, 2 * VDIM :].astype(f32) for k in range(XS)]
    for h in range(2):

        def whole(k, at):
            row = 6 * h + 3 * at
            return stats[k][row : row + 1] + stats[k][row + 1 : row + 2] + stats[k][row + 2 : row + 3]

        maxima = [whole(k, 0) for k in range(XS)]
        top = jnp.maximum(jnp.maximum(maxima[0], maxima[1]), jnp.maximum(maxima[2], maxima[3]))
        factors = [jnp.exp2(m - top) for m in maxima]
        total = sum(f * whole(k, 1) for k, f in enumerate(factors))
        numerator = sum(
            parts_ref[k, h * VDIM : (h + 1) * VDIM].astype(f32) * (f / total) for k, f in enumerate(factors)
        )
        out_ref[:, h * VDIM : (h + 1) * VDIM] = numerator.T.astype(bf16)


def call(kernel, out_shape, *args, scratch=()):
    return pl.pallas_call(
        kernel,
        out_shape=out_shape,
        in_specs=[pl.BlockSpec(memory_space=pltpu.VMEM)] * len(args),
        out_specs=jax.tree.map(lambda _: pl.BlockSpec(memory_space=pltpu.VMEM), out_shape),
        scratch_shapes=list(scratch),
        compiler_params=pltpu.CompilerParams(vmem_limit_bytes=VMEM_LIMIT),
    )(*args)


def pack_keys(latent):
    half = KEYS // 2
    rope = latent[:, D_LATENT:]
    return jnp.concatenate(
        [latent[:, :128], latent[:, 128:256], jnp.concatenate([rope[:half], rope[half:]], axis=1)], axis=0
    )


def pack_queries(queries, w_kv_up):
    wide = NOPE + ROPE
    return jnp.concatenate(
        [
            queries[:, :NOPE],
            queries[:, wide : wide + NOPE],
            jnp.concatenate([queries[:, NOPE:wide], queries[:, wide + NOPE :]], axis=1),
        ]
        + [w_kv_up[:, i * 128 : (i + 1) * 128] for i in range(4)],
        axis=0,
    )


def steps(queries, latent, w_kv_up):
    packed = pack_keys(latent)
    copies = jnp.broadcast_to(packed, (YS * ZS, PACKED, 128))
    mine = lax.all_to_all(copies, ("y", "z"), split_axis=0, concat_axis=0, tiled=True)
    rows = XS * UNIT
    state = (
        jax.ShapeDtypeStruct((1, rows), f32),
        jax.ShapeDtypeStruct((1, rows), f32),
        jax.ShapeDtypeStruct((D_LATENT, rows), f32),
    )
    own = pack_queries(queries, w_kv_up)
    qws = [own] + [
        lax.ppermute(own, "x", [(i, (i + k) % XS) for i in range(XS)]) for k in range(1, XS)
    ]
    shapes = (
        jax.ShapeDtypeStruct((768, rows), bf16),
        jax.ShapeDtypeStruct((2 * XS, VDIM, D_LATENT), bf16),
    )
    qcat, values = call(query_kernel, shapes, *qws)
    theirs = lax.ppermute(mine, "c", [(0, 1), (1, 0)])
    m, l, acc = call(first_kernel, state, mine, qcat)
    scratch = [pltpu.VMEM(s.shape, f32) for s in state]
    parts = call(
        second_kernel,
        jax.ShapeDtypeStruct((XS, OUT_ROWS, 128), bf16),
        values, theirs, qcat, m, l, acc,
        scratch=scratch,
    )
    parts = lax.all_to_all(parts, "x", split_axis=0, concat_axis=0, tiled=True)
    return call(combine_kernel, jax.ShapeDtypeStruct((GROUP, 2 * VDIM), bf16), parts)


def solution(mesh):
    mesh = Mesh(mesh.devices.reshape(YS, ZS, CS, XS), ("y", "z", "c", "x"))
    seq = ("y", "z", "c")
    in_specs = (P(seq, "x"), P((*seq, "x"), None), P(None, "x"))
    return jax.shard_map(steps, mesh=mesh, in_specs=in_specs, out_specs=P(seq, "x"), check_vma=False)
```

profile of v0, /device:TPU:56, one launch (start us, length us, event | category | flops | bytes accessed | tf_op | source)
XLA Modules:
  0.0 107.6 jit_solution(16289458000869205998)
XLA Ops:
  0.0 0.7 fusion.2
  0.7 0.7 fusion.1
  1.4 0.1 maximum_maximum_fusion
  1.5 1.3 %broadcast_in_dim.3 = bf16[64,80,128]{2,1,0:T(8,128)(2,1)} broadcast(bf16[80,128]{1,0:T(8,128)(2,1)S(1)} %maximum_maximum_fusion), dimensions={1,2} | broadcast | bytes 1331200 | tf_op jit(solution)/shard_map/broadcast_in_dim | solution.py:182
  2.8 16.3 %all-to-all-start = ((bf16[64,80,128]{2,1,0:T(8,128)(2,1)}), bf16[64,80,128]{2,1,0:T(8,128)(2,1)S(1)}, u32[]{:S(2)}, u32[]{:S(2)}) async-start(bf16[64,80,128]{2,1,0:T(8,128)(2,1)} %broadcast_in_dim.3), calls=%async_computation | async-start | bytes 2621440 | tf_op jit(solution)/shard_map/all_to_all | solution.py:183
  19.1 0.0 copy-done.1
  19.1 0.1 slice_dynamic-update-slice_fusion.4
  19.2 0.1 fusion
  19.3 33.9 %all-to-all-done.kv_ref = bf16[64,80,128]{2,1,0:T(8,128)(2,1)S(1)} async-done(((bf16[64,80,128]{2,1,0:T(8,128)(2,1)}), bf16[64,80,128]{2,1,0:T(8,128)(2,1)S(1)}, u32[]{:S(2)}, u32[]{:S(2)}) %all-to-all-start) | async-done | bytes 1310752 | tf_op jit(solution)/shard_map/all_to_all | solution.py:183
  53.1 1.9 %collective-permute-start.3 = (bf16[64,80,128]{2,1,0:T(8,128)(2,1)S(1)}, bf16[64,80,128]{2,1,0:T(8,128)(2,1)S(1)}, u32[]{:S(2)}, u32[]{:S(2)}) collective-permute-start(bf16[64,80,128]{2,1,0:T(8,128)(2,1)S(1)} %all-to-all-done.kv_ref), channel_id=1, source_target_pairs={{0,4},{4,0},{1,5},{5,1},{2,6},{6,2},{3,7},{7,3},{8,12},{12,8},{9,1... | collective-permute-start | bytes 3932168 | tf_op jit(solution)/shard_map/ppermute | solution.py:199
  55.0 0.1 maximum_dynamic-update-slice_fusion
  55.1 0.0 copy-done
  55.2 3.4 %collective-permute-start = (bf16[1408,128]{1,0:T(8,128)(2,1)S(1)}, bf16[1408,128]{1,0:T(8,128)(2,1)S(1)}, u32[]{:S(2)}, u32[]{:S(2)}) collective-permute-start(bf16[1408,128]{1,0:T(8,128)(2,1)S(1)} %slice_dynamic-update-slice_fusion.refs_0_), channel_id=1, source_target_pairs={{0,1},{1,2},{2,3},{3,0},{4,5},{5,6},{6,7},{7,4},{8,9},{9,10},{10,1... | collective-permute-start | bytes 1081352 | tf_op jit(solution)/shard_map/ppermute | solution.py:192
  58.6 4.6 %collective-permute-start.1 = (bf16[1408,128]{1,0:T(8,128)(2,1)S(1)}, bf16[1408,128]{1,0:T(8,128)(2,1)S(1)}, u32[]{:S(2)}, u32[]{:S(2)}) collective-permute-start(bf16[1408,128]{1,0:T(8,128)(2,1)S(1)} %slice_dynamic-update-slice_fusion.refs_0_), channel_id=1, source_target_pairs={{0,2},{1,3},{2,0},{3,1},{4,6},{5,7},{6,4},{7,5},{8,10},{9,11},{10,... | collective-permute-start | bytes 1081352 | tf_op jit(solution)/shard_map/ppermute | solution.py:192
  63.3 3.3 %collective-permute-start.2 = (bf16[1408,128]{1,0:T(8,128)(2,1)S(1)}, bf16[1408,128]{1,0:T(8,128)(2,1)S(1)}, u32[]{:S(2)}, u32[]{:S(2)}) collective-permute-start(bf16[1408,128]{1,0:T(8,128)(2,1)S(1)} %slice_dynamic-update-slice_fusion.refs_0_), channel_id=1, source_target_pairs={{0,3},{1,0},{2,1},{3,2},{4,7},{5,4},{6,5},{7,6},{8,11},{9,8},{10,9... | collective-permute-start | bytes 1081352 | tf_op jit(solution)/shard_map/ppermute | solution.py:192
  66.6 2.5 %collective-permute-done.refs_1_ = bf16[1408,128]{1,0:T(8,128)(2,1)S(1)} collective-permute-done((bf16[1408,128]{1,0:T(8,128)(2,1)S(1)}, bf16[1408,128]{1,0:T(8,128)(2,1)S(1)}, u32[]{:S(2)}, u32[]{:S(2)}) %collective-permute-start) | collective-permute-done | bytes 360480 | tf_op jit(solution)/shard_map/ppermute | solution.py:192
  69.2 8.7 %collective-permute-done.1.refs_2_ = bf16[1408,128]{1,0:T(8,128)(2,1)S(1)} collective-permute-done((bf16[1408,128]{1,0:T(8,128)(2,1)S(1)}, bf16[1408,128]{1,0:T(8,128)(2,1)S(1)}, u32[]{:S(2)}, u32[]{:S(2)}) %collective-permute-start.1) | collective-permute-done | bytes 360480 | tf_op jit(solution)/shard_map/ppermute | solution.py:192
  77.9 1.6 %collective-permute-done.2.refs_3_ = bf16[1408,128]{1,0:T(8,128)(2,1)S(1)} collective-permute-done((bf16[1408,128]{1,0:T(8,128)(2,1)S(1)}, bf16[1408,128]{1,0:T(8,128)(2,1)S(1)}, u32[]{:S(2)}, u32[]{:S(2)}) %collective-permute-start.2) | collective-permute-done | bytes 360480 | tf_op jit(solution)/shard_map/ppermute | solution.py:192
  79.4 0.5 shard_map.37
  79.9 7.8 %shard_map.38 = (f32[1,1024]{1,0:T(1,128)S(1)}, f32[1,1024]{1,0:T(1,128)S(1)}, f32[256,1024]{1,0:T(8,128)S(1)}) custom-call(bf16[64,80,128]{2,1,0:T(8,128)(2,1)S(1)} %all-to-all-done.kv_ref, bf16[768,1024]{1,0:T(8,128)(2,1)S(1)} %get-tuple-element.11.qcat_ref), custom_call_target="tpu_custom_call" | custom-call | tf_op jit(solution)/shard_map/pallas_call | solution.py:149
  87.7 0.0 collective-permute-done.3.kv_ref
  87.7 8.2 %shard_map.39 = bf16[4,272,128]{2,1,0:T(8,128)(2,1)S(1)} custom-call(bf16[8,128,256]{2,1,0:T(8,128)(2,1)S(1)} %get-tuple-element.10.values_ref, bf16[64,80,128]{2,1,0:T(8,128)(2,1)S(1)} %collective-permute-done.3.kv_ref, bf16[768,1024]{1,0:T(8,128)(2,1)S(1)} %get-tuple-element.11.qcat_ref, f32[1,1024]{1,0:T(1,128)S(1)} %get-tuple-element.12.m_in, ...), custom_call_target="tpu_custom_call" | custom-call | tf_op jit(solution)/shard_map/pallas_call | solution.py:149
  95.9 10.8 %all_to_all.10.parts_ref = bf16[4,272,128]{2,1,0:T(8,128)(2,1)S(1)} all-to-all(bf16[4,272,128]{2,1,0:T(8,128)(2,1)S(1)} %shard_map.39), channel_id=1, replica_groups=mesh['y'=8,'z'=8,'c'=2,'x'=4] {'x'}, dimensions={0} | all-to-all | bytes 557056 | tf_op jit(solution)/shard_map/all_to_all | solution.py:208
  106.8 0.8 shard_map.40
  (7 shorter events, 0.1 us)
Async XLA Ops:
  2.8 16.3 %copy-start.1 = (bf16[128,384]{1,0:T(8,128)(2,1)S(1)}, bf16[128,384]{1,0:T(8,128)(2,1)}, u32[]{:S(2)}) copy-start(bf16[128,384]{1,0:T(8,128)(2,1)} %param.3) | copy-start | bytes 294916
  2.8 52.4 %copy-start = (bf16[256,512]{1,0:T(8,128)(2,1)S(1)}, bf16[256,512]{1,0:T(8,128)(2,1)}, u32[]{:S(2)}) copy-start(bf16[256,512]{1,0:T(8,128)(2,1)} %param.5) | copy-start | bytes 786436
  2.8 50.4 %all-to-all-start = ((bf16[64,80,128]{2,1,0:T(8,128)(2,1)}), bf16[64,80,128]{2,1,0:T(8,128)(2,1)S(1)}, u32[]{:S(2)}, u32[]{:S(2)}) async-start(bf16[64,80,128]{2,1,0:T(8,128)(2,1)} %broadcast_in_dim.3), calls=%async_computation | async-start | bytes 2621440 | tf_op jit(solution)/shard_map/all_to_all | solution.py:183
  53.1 34.6 %collective-permute-start.3 = (bf16[64,80,128]{2,1,0:T(8,128)(2,1)S(1)}, bf16[64,80,128]{2,1,0:T(8,128)(2,1)S(1)}, u32[]{:S(2)}, u32[]{:S(2)}) collective-permute-start(bf16[64,80,128]{2,1,0:T(8,128)(2,1)S(1)} %all-to-all-done.kv_ref), channel_id=1, source_target_pairs={{0,4},{4,0},{1,5},{5,1},{2,6},{6,2},{3,7},{7,3},{8,12},{12,8},{9,1... | collective-permute-start | bytes 3932168 | tf_op jit(solution)/shard_map/ppermute | solution.py:199
  55.2 13.9 %collective-permute-start = (bf16[1408,128]{1,0:T(8,128)(2,1)S(1)}, bf16[1408,128]{1,0:T(8,128)(2,1)S(1)}, u32[]{:S(2)}, u32[]{:S(2)}) collective-permute-start(bf16[1408,128]{1,0:T(8,128)(2,1)S(1)} %slice_dynamic-update-slice_fusion.refs_0_), channel_id=1, source_target_pairs={{0,1},{1,2},{2,3},{3,0},{4,5},{5,6},{6,7},{7,4},{8,9},{9,10},{10,1... | collective-permute-start | bytes 1081352 | tf_op jit(solution)/shard_map/ppermute | solution.py:192
  58.6 19.2 %collective-permute-start.1 = (bf16[1408,128]{1,0:T(8,128)(2,1)S(1)}, bf16[1408,128]{1,0:T(8,128)(2,1)S(1)}, u32[]{:S(2)}, u32[]{:S(2)}) collective-permute-start(bf16[1408,128]{1,0:T(8,128)(2,1)S(1)} %slice_dynamic-update-slice_fusion.refs_0_), channel_id=1, source_target_pairs={{0,2},{1,3},{2,0},{3,1},{4,6},{5,7},{6,4},{7,5},{8,10},{9,11},{10,... | collective-permute-start | bytes 1081352 | tf_op jit(solution)/shard_map/ppermute | solution.py:192
  63.3 16.1 %collective-permute-start.2 = (bf16[1408,128]{1,0:T(8,128)(2,1)S(1)}, bf16[1408,128]{1,0:T(8,128)(2,1)S(1)}, u32[]{:S(2)}, u32[]{:S(2)}) collective-permute-start(bf16[1408,128]{1,0:T(8,128)(2,1)S(1)} %slice_dynamic-update-slice_fusion.refs_0_), channel_id=1, source_target_pairs={{0,3},{1,0},{2,1},{3,2},{4,7},{5,4},{6,5},{7,6},{8,11},{9,8},{10,9... | collective-permute-start | bytes 1081352 | tf_op jit(solution)/shard_map/ppermute | solution.py:192
where the time goes:
time: 108 us
  waiting for transfers between devices  46.6 us (43%)
  starting transfers between devices  29.6 us (27%)
  Pallas kernels  17.3 us (16%)
  blocking collectives  10.8 us (10%)
  local copies, waits for them, and re-layouts  2.94 us (3%)
    all_to_all x1, waiting for transfers between devices, steps(): lax.all_to_all(copies, ('y', 'z'), split_axis=0, concat_axis=0, tiled=True)  33.9 us
    pallas_call x4, Pallas kernels, call(): pl.pallas_call(kernel, out_shape=out_shape, in_specs=[pl.BlockSpec(memory...  17.3 us
    all_to_all x1, starting transfers between devices, steps(): lax.all_to_all(copies, ('y', 'z'), split_axis=0, concat_axis=0, tiled=True)  16.3 us
    ppermute x3, waiting for transfers between devices, steps(): lax.ppermute(own, 'x', [(i, (i + k) % XS) for i in range(XS)])  12.8 us
    ppermute x3, starting transfers between devices, steps(): lax.ppermute(own, 'x', [(i, (i + k) % XS) for i in range(XS)])  11.4 us
    all_to_all x1, blocking collectives, steps(): parts = lax.all_to_all(parts, 'x', split_axis=0, concat_axis=0, tiled=True)  10.8 us
  transfers between devices with their start and end apart: 5, of which 4 were waited for; matrix products, arithmetic and copies ran while one was open for 0% of the time, Pallas kernels for 8%

commit v1 on v0

--- a/solution.py
+++ b/solution.py
@@ -1,3 +1,4 @@
+import functools
 import math
 
 import jax
@@ -13,14 +14,16 @@
 NOPE = 128
 VDIM = 128
 MASKED = -1e30
+LOWEST = -0.5e30
 LOG2_SCALE = math.log2(math.e) * (NOPE + ROPE) ** -0.5
 
 
-YS, ZS, CS, XS = 8, 8, 2, 4
+YS, ZH, ZL, CS, XS = 8, 4, 2, 2, 4
 GROUP = 128
 KEYS = 32
 UNIT = 2 * GROUP
-CHUNK = ZS * KEYS
+SPAN = 4
+CHUNK = SPAN * ZH * KEYS
 PACKED = KEYS * (D_LATENT + ROPE) // 128
 VMEM_LIMIT = 20 * 2**20
 OUT_ROWS = 2 * VDIM + 16
@@ -53,8 +56,8 @@
             qcat_ref[512:768, cols] = jnp.concatenate([high, none, low, none], axis=0)
 
 
-def one_chunk(kv_ref, row, masks, qcat_ref, m_ref, l_ref, acc_ref):
-    block = kv_ref[pl.ds(row * ZS, ZS)]
+def one_chunk(kv_ref, index, allowed, qcat_ref, m_ref, l_ref, acc_ref):
+    block = kv_ref[pl.ds(index * SPAN * ZH, SPAN * ZH)]
     latent = jnp.concatenate(
         [block[:, 0:KEYS].reshape(CHUNK, 128), block[:, KEYS : 2 * KEYS].reshape(CHUNK, 128)], axis=1
     )
@@ -65,39 +68,46 @@
     turned = latent.T
     units = [pl.ds(u * UNIT, UNIT) for u in range(XS)]
     scores = [jnp.dot(keys, qcat_ref[:, cols], preferred_element_type=f32) for cols in units]
-    for u, cols in enumerate(units):
-        s = scores[u]
-        if masks is not None:
-            s = jnp.where(masks, s, MASKED)
+    for s, cols in zip(scores, units):
+        if allowed is not None:
+            s = jnp.where(allowed, s, MASKED)
         m_old = m_ref[:, cols]
         m_new = jnp.maximum(m_old, jnp.max(s, axis=0, keepdims=True))
         factor = jnp.exp2(m_old - m_new)
         weights = jnp.exp2(s - m_new)
-        if masks is not None:
-            weights = jnp.where(masks, weights, 0.0)
         l_ref[:, cols] = l_ref[:, cols] * factor + jnp.sum(weights, axis=0, keepdims=True)
         m_ref[:, cols] = m_new
         update = jnp.dot(turned, weights.astype(bf16), preferred_element_type=f32)
         acc_ref[:, cols] = acc_ref[:, cols] * factor + update
 
 
-def attend(kv_ref, from_other, qcat_ref, m_ref, l_ref, acc_ref):
-    y, z, c, x = (lax.axis_index(a) for a in ("y", "z", "c", "x"))
-    key_core = 1 - c if from_other else c
+def attend(kv_ref, same_parity, same_core, qcat_ref, m_ref, l_ref, acc_ref):
+    y, zh, zl, c, x = (lax.axis_index(a) for a in ("y", "zh", "zl", "c", "x"))
+    key_zl = zl if same_parity else 1 - zl
+    key_c = c if same_core else 1 - c
+    last = y // SPAN
     key = lax.broadcasted_iota(jnp.int32, (CHUNK, UNIT), 0)
     row = lax.broadcasted_iota(jnp.int32, (CHUNK, UNIT), 1) % GROUP
-    query_pos = (z * 2 + c) * GROUP + row
-    key_pos = ((key // KEYS) * 2 + key_core) * GROUP + x * KEYS + key % KEYS
+    query_pos = (((y * ZH + zh) * ZL + zl) * CS + c) * GROUP + row
+    key_group = ((last * SPAN * ZH + key // KEYS) * ZL + key_zl) * CS + key_c
+    key_pos = key_group * GROUP + x * KEYS + key % KEYS
     refs = (qcat_ref, m_ref, l_ref, acc_ref)
-    one_chunk(kv_ref, y, key_pos <= query_pos, *refs)
-    lax.fori_loop(0, y, lambda i, _: one_chunk(kv_ref, i, None, *refs), None)
-
-
-def first_kernel(kv_ref, qcat_ref, m_ref, l_ref, acc_ref):
-    m_ref[...] = jnp.full(m_ref.shape, MASKED, f32)
+    one_chunk(kv_ref, last, key_pos <= query_pos, *refs)
+    lax.fori_loop(0, last, lambda i, _: one_chunk(kv_ref, i, None, *refs), None)
+
+
+def attend_first(kv_ref, qcat_ref, m_ref, l_ref, acc_ref):
+    m_ref[...] = jnp.full(m_ref.shape, LOWEST, f32)
     l_ref[...] = jnp.zeros(l_ref.shape, f32)
     acc_ref[...] = jnp.zeros(acc_ref.shape, f32)
-    attend(kv_ref, False, qcat_ref, m_ref, l_ref, acc_ref)
+    attend(kv_ref, True, True, qcat_ref, m_ref, l_ref, acc_ref)
+
+
+def attend_more(same_parity, same_core, kv_ref, qcat_ref, m_in, l_in, acc_in, m_ref, l_ref, acc_ref):
+    m_ref[...] = m_in[...]
+    l_ref[...] = l_in[...]
+    acc_ref[...] = acc_in[...]
+    attend(kv_ref, same_parity, same_core, qcat_ref, m_ref, l_ref, acc_ref)
 
 
 def thirds(value):
@@ -106,11 +116,8 @@
     return [high, middle, low]
 
 
-def second_kernel(values_ref, kv_ref, qcat_ref, m_in, l_in, acc_in, out_ref, m_ref, l_ref, acc_ref):
-    m_ref[...] = m_in[...]
-    l_ref[...] = l_in[...]
-    acc_ref[...] = acc_in[...]
-    attend(kv_ref, True, qcat_ref, m_ref, l_ref, acc_ref)
+def attend_last(values_ref, kv_ref, qcat_ref, m_in, l_in, acc_in, out_ref, m_ref, l_ref, acc_ref):
+    attend_more(False, False, kv_ref, qcat_ref, m_in, l_in, acc_in, m_ref, l_ref, acc_ref)
     x = lax.axis_index("x")
     for k in range(XS):
         owner = lax.rem(x + XS - k, XS)
@@ -156,12 +163,13 @@
     )(*args)
 
 
-def pack_keys(latent):
+def pack_kernel(latent_ref, out_ref):
     half = KEYS // 2
-    rope = latent[:, D_LATENT:]
-    return jnp.concatenate(
-        [latent[:, :128], latent[:, 128:256], jnp.concatenate([rope[:half], rope[half:]], axis=1)], axis=0
-    )
+    rows = latent_ref[...].astype(f32)
+    rope = jnp.concatenate([rows[:half, D_LATENT:], rows[half:, D_LATENT:]], axis=1)
+    packed = jnp.concatenate([rows[:, :128], rows[:, 128:256], rope], axis=0).astype(bf16)
+    for i in range(YS * ZH):
+        out_ref[i] = packed
 
 
 def pack_queries(queries, w_kv_up):
@@ -178,9 +186,8 @@
 
 
 def steps(queries, latent, w_kv_up):
-    packed = pack_keys(latent)
-    copies = jnp.broadcast_to(packed, (YS * ZS, PACKED, 128))
-    mine = lax.all_to_all(copies, ("y", "z"), split_axis=0, concat_axis=0, tiled=True)
+    copies = call(pack_kernel, jax.ShapeDtypeStruct((YS * ZH, PACKED, 128), bf16), latent)
+    near = lax.all_to_all(copies, ("y", "zh"), split_axis=0, concat_axis=0, tiled=True)
     rows = XS * UNIT
     state = (
         jax.ShapeDtypeStruct((1, rows), f32),
@@ -196,21 +203,28 @@
         jax.ShapeDtypeStruct((2 * XS, VDIM, D_LATENT), bf16),
     )
     qcat, values = call(query_kernel, shapes, *qws)
-    theirs = lax.ppermute(mine, "c", [(0, 1), (1, 0)])
-    m, l, acc = call(first_kernel, state, mine, qcat)
-    scratch = [pltpu.VMEM(s.shape, f32) for s in state]
+    zs, middle = ZH * ZL, YS * ZH // 2
+    low = lax.ppermute(near[:middle], ("zh", "zl"), [(i, (i + 1) % zs) for i in range(zs)])
+    high = lax.ppermute(near[middle:], ("zh", "zl"), [(i, (i - 1) % zs) for i in range(zs)])
+    swap = [(0, 1), (1, 0)]
+    near_other = lax.ppermute(near, "c", swap)
+    m, l, acc = call(attend_first, state, near, qcat)
+    m, l, acc = call(functools.partial(attend_more, True, False), state, near_other, qcat, m, l, acc)
+    far = jnp.concatenate([low, high])
+    far_other = lax.ppermute(far, "c", swap)
+    m, l, acc = call(functools.partial(attend_more, False, True), state, far, qcat, m, l, acc)
     parts = call(
-        second_kernel,
+        attend_last,
         jax.ShapeDtypeStruct((XS, OUT_ROWS, 128), bf16),
-        values, theirs, qcat, m, l, acc,
-        scratch=scratch,
+        values, far_other, qcat, m, l, acc,
+        scratch=[pltpu.VMEM(s.shape, f32) for s in state],
     )
     parts = lax.all_to_all(parts, "x", split_axis=0, concat_axis=0, tiled=True)
     return call(combine_kernel, jax.ShapeDtypeStruct((GROUP, 2 * VDIM), bf16), parts)
 
 
 def solution(mesh):
-    mesh = Mesh(mesh.devices.reshape(YS, ZS, CS, XS), ("y", "z", "c", "x"))
-    seq = ("y", "z", "c")
+    mesh = Mesh(mesh.devices.reshape(YS, ZH, ZL, CS, XS), ("y", "zh", "zl", "c", "x"))
+    seq = ("y", "zh", "zl", "c")
     in_specs = (P(seq, "x"), P((*seq, "x"), None), P(None, "x"))
     return jax.shard_map(steps, mesh=mesh, in_specs=in_specs, out_specs=P(seq, "x"), check_vma=False)

time: 108 us -> 102 us (0.944)
  the two profiles are of different devices: /device:TPU:56 before, /device:TPU:48 now
where the time goes in v1:
time: 102 us; the launch traced here: 101 us
  starting transfers between devices  38.1 us (37%)
  waiting for transfers between devices  36 us (35%)
  Pallas kernels  15.1 us (15%)
  blocking collectives  10.9 us (11%)
  local copies, waits for them, and re-layouts  1.11 us (1%)
    all_to_all x1, waiting for transfers between devices, steps(): lax.all_to_all(copies, ('y', 'zh'), split_axis=0, concat_axis=0, tiled=True)  19.2 us
    all_to_all x1, starting transfers between devices, steps(): lax.all_to_all(copies, ('y', 'zh'), split_axis=0, concat_axis=0, tiled=True)  15.8 us
    pallas_call x7, Pallas kernels, call(): pl.pallas_call(kernel, out_shape=out_shape, in_specs=[pl.BlockSpec(memory...  15.1 us
    ppermute x3, waiting for transfers between devices, steps(): lax.ppermute(own, 'x', [(i, (i + k) % XS) for i in range(XS)])  12.8 us
    ppermute x3, starting transfers between devices, steps(): lax.ppermute(own, 'x', [(i, (i + k) % XS) for i in range(XS)])  11.4 us
    all_to_all x1, blocking collectives, steps(): parts = lax.all_to_all(parts, 'x', split_axis=0, concat_axis=0, tiled=True)  10.9 us
    ppermute x1, starting transfers between devices, steps(): lax.ppermute(near[:middle], ('zh', 'zl'), [(i, (i + 1) % zs) for i in ran...  3.77 us
    ppermute x1, starting transfers between devices, steps(): lax.ppermute(near[middle:], ('zh', 'zl'), [(i, (i - 1) % zs) for i in ran...  3.28 us
  transfers between devices with their start and end apart: 8, of which 6 were waited for; matrix products, arithmetic and copies ran while one was open for 0% of the time, Pallas kernels for 10%

profile of v1, /device:TPU:48, one launch (start us, length us, event | category | flops | bytes accessed | tf_op | source)
XLA Modules:
  0.0 101.3 jit_solution(14128403423965213844)
XLA Ops:
  0.0 0.7 copy-done
  0.7 0.9 shard_map.38
  1.7 15.8 %all-to-all-start = ((bf16[32,80,128]{2,1,0:T(8,128)(2,1)}), bf16[32,80,128]{2,1,0:T(8,128)(2,1)S(1)}, u32[]{:S(2)}, u32[]{:S(2)}) async-start(bf16[32,80,128]{2,1,0:T(8,128)(2,1)} %shard_map.38), calls=%async_computation | async-start | bytes 1310720 | tf_op jit(solution)/shard_map/all_to_all | solution.py:190
  17.7 0.1 maximum_dynamic-update-slice_fusion
  17.7 19.2 %all-to-all-done.kv_ref = bf16[32,80,128]{2,1,0:T(8,128)(2,1)S(1)} async-done(((bf16[32,80,128]{2,1,0:T(8,128)(2,1)}), bf16[32,80,128]{2,1,0:T(8,128)(2,1)S(1)}, u32[]{:S(2)}, u32[]{:S(2)}) %all-to-all-start) | async-done | bytes 655392 | tf_op jit(solution)/shard_map/all_to_all | solution.py:190
  37.0 3.8 %collective-permute-start.3 = (bf16[16,80,128]{2,1,0:T(8,128)(2,1)S(1)}, bf16[16,80,128]{2,1,0:T(8,128)(2,1)S(1)}, u32[]{:S(2)}, u32[]{:S(2)}) collective-permute-start(bf16[16,80,128]{2,1,0:T(8,128)(2,1)S(1)} %get-tuple-element.28), channel_id=1, source_target_pairs={{0,8},{8,16},{16,24},{24,32},{32,40},{40,48},{48,56},{56,0},{1,9},... | collective-permute-start | bytes 983048 | tf_op jit(solution)/shard_map/ppermute | solution.py:207
  40.8 3.3 %collective-permute-start.4 = (bf16[16,80,128]{2,1,0:T(8,128)(2,1)S(1)}, bf16[16,80,128]{2,1,0:T(8,128)(2,1)S(1)}, u32[]{:S(2)}, u32[]{:S(2)}) collective-permute-start(bf16[16,80,128]{2,1,0:T(8,128)(2,1)S(1)} %get-tuple-element.27), channel_id=1, source_target_pairs={{0,56},{8,0},{16,8},{24,16},{32,24},{40,32},{48,40},{56,48},{1,57}... | collective-permute-start | bytes 983048 | tf_op jit(solution)/shard_map/ppermute | solution.py:208
  44.1 1.9 %collective-permute-start.6 = (bf16[32,80,128]{2,1,0:T(8,128)(2,1)S(1)}, bf16[32,80,128]{2,1,0:T(8,128)(2,1)S(1)}, u32[]{:S(2)}, u32[]{:S(2)}) collective-permute-start(bf16[32,80,128]{2,1,0:T(8,128)(2,1)S(1)} %all-to-all-done.kv_ref), channel_id=1, source_target_pairs={{0,4},{4,0},{1,5},{5,1},{2,6},{6,2},{3,7},{7,3},{8,12},{12,8},{9,1... | collective-permute-start | bytes 1966088 | tf_op jit(solution)/shard_map/ppermute | solution.py:210
  46.1 2.2 %collective-permute-done.3 = bf16[16,80,128]{2,1,0:T(8,128)(2,1)S(1)} collective-permute-done((bf16[16,80,128]{2,1,0:T(8,128)(2,1)S(1)}, bf16[16,80,128]{2,1,0:T(8,128)(2,1)S(1)}, u32[]{:S(2)}, u32[]{:S(2)}) %collective-permute-start.3) | collective-permute-done | bytes 327712 | tf_op jit(solution)/shard_map/ppermute | solution.py:207
  48.2 1.8 %collective-permute-done.4 = bf16[16,80,128]{2,1,0:T(8,128)(2,1)S(1)} collective-permute-done((bf16[16,80,128]{2,1,0:T(8,128)(2,1)S(1)}, bf16[16,80,128]{2,1,0:T(8,128)(2,1)S(1)}, u32[]{:S(2)}, u32[]{:S(2)}) %collective-permute-start.4) | collective-permute-done | bytes 327712 | tf_op jit(solution)/shard_map/ppermute | solution.py:208
  50.1 1.9 %collective-permute-start.5 = (bf16[32,80,128]{2,1,0:T(8,128)(2,1)S(1)}, bf16[32,80,128]{2,1,0:T(8,128)(2,1)S(1)}, u32[]{:S(2)}, u32[]{:S(2)}) collective-permute-start(bf16[32,80,128]{2,1,0:T(8,128)(2,1)S(1)} %constant_dynamic-update-slice_fusion.kv_ref), channel_id=1, source_target_pairs={{0,4},{4,0},{1,5},{5,1},{2,6},{6,2},{3,7},{7,3},{8,12},{12,8},{9,1... | collective-permute-start | bytes 1966088 | tf_op jit(solution)/shard_map/ppermute | solution.py:214
  52.1 3.4 %collective-permute-start = (bf16[1408,128]{1,0:T(8,128)(2,1)S(1)}, bf16[1408,128]{1,0:T(8,128)(2,1)S(1)}, u32[]{:S(2)}, u32[]{:S(2)}) collective-permute-start(bf16[1408,128]{1,0:T(8,128)(2,1)S(1)} %slice_dynamic-update-slice_fusion.refs_0_), channel_id=1, source_target_pairs={{0,1},{1,2},{2,3},{3,0},{4,5},{5,6},{6,7},{7,4},{8,9},{9,10},{10,1... | collective-permute-start | bytes 1081352 | tf_op jit(solution)/shard_map/ppermute | solution.py:199
  55.5 4.6 %collective-permute-start.1 = (bf16[1408,128]{1,0:T(8,128)(2,1)S(1)}, bf16[1408,128]{1,0:T(8,128)(2,1)S(1)}, u32[]{:S(2)}, u32[]{:S(2)}) collective-permute-start(bf16[1408,128]{1,0:T(8,128)(2,1)S(1)} %slice_dynamic-update-slice_fusion.refs_0_), channel_id=1, source_target_pairs={{0,2},{1,3},{2,0},{3,1},{4,6},{5,7},{6,4},{7,5},{8,10},{9,11},{10,... | collective-permute-start | bytes 1081352 | tf_op jit(solution)/shard_map/ppermute | solution.py:199
  60.1 3.3 %collective-permute-start.2 = (bf16[1408,128]{1,0:T(8,128)(2,1)S(1)}, bf16[1408,128]{1,0:T(8,128)(2,1)S(1)}, u32[]{:S(2)}, u32[]{:S(2)}) collective-permute-start(bf16[1408,128]{1,0:T(8,128)(2,1)S(1)} %slice_dynamic-update-slice_fusion.refs_0_), channel_id=1, source_target_pairs={{0,3},{1,0},{2,1},{3,2},{4,7},{5,4},{6,5},{7,6},{8,11},{9,8},{10,9... | collective-permute-start | bytes 1081352 | tf_op jit(solution)/shard_map/ppermute | solution.py:199
  63.5 2.5 %collective-permute-done.refs_1_ = bf16[1408,128]{1,0:T(8,128)(2,1)S(1)} collective-permute-done((bf16[1408,128]{1,0:T(8,128)(2,1)S(1)}, bf16[1408,128]{1,0:T(8,128)(2,1)S(1)}, u32[]{:S(2)}, u32[]{:S(2)}) %collective-permute-start) | collective-permute-done | bytes 360480 | tf_op jit(solution)/shard_map/ppermute | solution.py:199
  66.0 8.7 %collective-permute-done.1.refs_2_ = bf16[1408,128]{1,0:T(8,128)(2,1)S(1)} collective-permute-done((bf16[1408,128]{1,0:T(8,128)(2,1)S(1)}, bf16[1408,128]{1,0:T(8,128)(2,1)S(1)}, u32[]{:S(2)}, u32[]{:S(2)}) %collective-permute-start.1) | collective-permute-done | bytes 360480 | tf_op jit(solution)/shard_map/ppermute | solution.py:199
  74.7 1.6 %collective-permute-done.2.refs_3_ = bf16[1408,128]{1,0:T(8,128)(2,1)S(1)} collective-permute-done((bf16[1408,128]{1,0:T(8,128)(2,1)S(1)}, bf16[1408,128]{1,0:T(8,128)(2,1)S(1)}, u32[]{:S(2)}, u32[]{:S(2)}) %collective-permute-start.2) | collective-permute-done | bytes 360480 | tf_op jit(solution)/shard_map/ppermute | solution.py:199
  76.3 0.4 shard_map.37
  76.7 3.1 %shard_map.39 = (f32[1,1024]{1,0:T(1,128)S(1)}, f32[1,1024]{1,0:T(1,128)S(1)}, f32[256,1024]{1,0:T(8,128)S(1)}) custom-call(bf16[32,80,128]{2,1,0:T(8,128)(2,1)S(1)} %all-to-all-done.kv_ref, bf16[768,1024]{1,0:T(8,128)(2,1)S(1)} %get-tuple-element.17.qcat_ref), custom_call_target="tpu_custom_call" | custom-call | tf_op jit(solution)/shard_map/pallas_call | solution.py:156
  79.9 3.1 %shard_map.40 = (f32[1,1024]{1,0:T(1,128)S(1)}, f32[1,1024]{1,0:T(1,128)S(1)}, f32[256,1024]{1,0:T(8,128)S(1)}) custom-call(bf16[32,80,128]{2,1,0:T(8,128)(2,1)S(1)} %collective-permute-done.6.kv_ref, bf16[768,1024]{1,0:T(8,128)(2,1)S(1)} %get-tuple-element.17.qcat_ref, f32[1,1024]{1,0:T(1,128)S(1)} %get-tuple-element.18.m_in, ...), custom_call_target="tpu_custom_call" | custom-call | tf_op jit(solution)/shard_map/pallas_call | solution.py:156
  83.0 3.1 %shard_map.41 = (f32[1,1024]{1,0:T(1,128)S(1)}, f32[1,1024]{1,0:T(1,128)S(1)}, f32[256,1024]{1,0:T(8,128)S(1)}) custom-call(bf16[32,80,128]{2,1,0:T(8,128)(2,1)S(1)} %constant_dynamic-update-slice_fusion.kv_ref, bf16[768,1024]{1,0:T(8,128)(2,1)S(1)} %get-tuple-element.17.qcat_ref, f32[1,1024]{1,0:T(1,128)S(1)} %get-tuple-element.21.m_in, ...), custom_call_target="tpu_custom_call" | custom-call | tf_op jit(solution)/shard_map/pallas_call | solution.py:156
  86.1 3.6 %shard_map.42 = bf16[4,272,128]{2,1,0:T(8,128)(2,1)S(1)} custom-call(bf16[8,128,256]{2,1,0:T(8,128)(2,1)S(1)} %get-tuple-element.16.values_ref, bf16[32,80,128]{2,1,0:T(8,128)(2,1)S(1)} %collective-permute-done.5.kv_ref, bf16[768,1024]{1,0:T(8,128)(2,1)S(1)} %get-tuple-element.17.qcat_ref, f32[1,1024]{1,0:T(1,128)S(1)} %get-tuple-element.24.m_in, ...), custom_call_target="tpu_custom_call" | custom-call | tf_op jit(solution)/shard_map/pallas_call | solution.py:156
  89.7 10.9 %all_to_all.10.parts_ref = bf16[4,272,128]{2,1,0:T(8,128)(2,1)S(1)} all-to-all(bf16[4,272,128]{2,1,0:T(8,128)(2,1)S(1)} %shard_map.42), channel_id=1, replica_groups=mesh['y'=8,'zh'=4,'zl'=2,'c'=2,'x'=4] {'x'}, dimensions={0} | all-to-all | bytes 557056 | tf_op jit(solution)/shard_map/all_to_all | solution.py:222
  100.6 0.8 shard_map.43
  (17 shorter events, 0.4 us)
Async XLA Ops:
  0.0 0.7 copy-start
  0.7 16.7 %copy-start.2 = (bf16[128,384]{1,0:T(8,128)(2,1)S(1)}, bf16[128,384]{1,0:T(8,128)(2,1)}, u32[]{:S(2)}) copy-start(bf16[128,384]{1,0:T(8,128)(2,1)} %param.3) | copy-start | bytes 294916
  1.7 39.1 %copy-start.1 = (bf16[256,512]{1,0:T(8,128)(2,1)S(1)}, bf16[256,512]{1,0:T(8,128)(2,1)}, u32[]{:S(2)}) copy-start(bf16[256,512]{1,0:T(8,128)(2,1)} %param.5) | copy-start | bytes 786436
  1.7 35.3 %all-to-all-start = ((bf16[32,80,128]{2,1,0:T(8,128)(2,1)}), bf16[32,80,128]{2,1,0:T(8,128)(2,1)S(1)}, u32[]{:S(2)}, u32[]{:S(2)}) async-start(bf16[32,80,128]{2,1,0:T(8,128)(2,1)} %shard_map.38), calls=%async_computation | async-start | bytes 1310720 | tf_op jit(solution)/shard_map/all_to_all | solution.py:190
  37.0 11.2 %collective-permute-start.3 = (bf16[16,80,128]{2,1,0:T(8,128)(2,1)S(1)}, bf16[16,80,128]{2,1,0:T(8,128)(2,1)S(1)}, u32[]{:S(2)}, u32[]{:S(2)}) collective-permute-start(bf16[16,80,128]{2,1,0:T(8,128)(2,1)S(1)} %get-tuple-element.28), channel_id=1, source_target_pairs={{0,8},{8,16},{16,24},{24,32},{32,40},{40,48},{48,56},{56,0},{1,9},... | collective-permute-start | bytes 983048 | tf_op jit(solution)/shard_map/ppermute | solution.py:207
  40.8 9.3 %collective-permute-start.4 = (bf16[16,80,128]{2,1,0:T(8,128)(2,1)S(1)}, bf16[16,80,128]{2,1,0:T(8,128)(2,1)S(1)}, u32[]{:S(2)}, u32[]{:S(2)}) collective-permute-start(bf16[16,80,128]{2,1,0:T(8,128)(2,1)S(1)} %get-tuple-element.27), channel_id=1, source_target_pairs={{0,56},{8,0},{16,8},{24,16},{32,24},{40,32},{48,40},{56,48},{1,57}... | collective-permute-start | bytes 983048 | tf_op jit(solution)/shard_map/ppermute | solution.py:208
  44.1 35.7 %collective-permute-start.6 = (bf16[32,80,128]{2,1,0:T(8,128)(2,1)S(1)}, bf16[32,80,128]{2,1,0:T(8,128)(2,1)S(1)}, u32[]{:S(2)}, u32[]{:S(2)}) collective-permute-start(bf16[32,80,128]{2,1,0:T(8,128)(2,1)S(1)} %all-to-all-done.kv_ref), channel_id=1, source_target_pairs={{0,4},{4,0},{1,5},{5,1},{2,6},{6,2},{3,7},{7,3},{8,12},{12,8},{9,1... | collective-permute-start | bytes 1966088 | tf_op jit(solution)/shard_map/ppermute | solution.py:210
  50.1 36.0 %collective-permute-start.5 = (bf16[32,80,128]{2,1,0:T(8,128)(2,1)S(1)}, bf16[32,80,128]{2,1,0:T(8,128)(2,1)S(1)}, u32[]{:S(2)}, u32[]{:S(2)}) collective-permute-start(bf16[32,80,128]{2,1,0:T(8,128)(2,1)S(1)} %constant_dynamic-update-slice_fusion.kv_ref), channel_id=1, source_target_pairs={{0,4},{4,0},{1,5},{5,1},{2,6},{6,2},{3,7},{7,3},{8,12},{12,8},{9,1... | collective-permute-start | bytes 1966088 | tf_op jit(solution)/shard_map/ppermute | solution.py:214
  52.1 13.9 %collective-permute-start = (bf16[1408,128]{1,0:T(8,128)(2,1)S(1)}, bf16[1408,128]{1,0:T(8,128)(2,1)S(1)}, u32[]{:S(2)}, u32[]{:S(2)}) collective-permute-start(bf16[1408,128]{1,0:T(8,128)(2,1)S(1)} %slice_dynamic-update-slice_fusion.refs_0_), channel_id=1, source_target_pairs={{0,1},{1,2},{2,3},{3,0},{4,5},{5,6},{6,7},{7,4},{8,9},{9,10},{10,1... | collective-permute-start | bytes 1081352 | tf_op jit(solution)/shard_map/ppermute | solution.py:199
  55.5 19.2 %collective-permute-start.1 = (bf16[1408,128]{1,0:T(8,128)(2,1)S(1)}, bf16[1408,128]{1,0:T(8,128)(2,1)S(1)}, u32[]{:S(2)}, u32[]{:S(2)}) collective-permute-start(bf16[1408,128]{1,0:T(8,128)(2,1)S(1)} %slice_dynamic-update-slice_fusion.refs_0_), channel_id=1, source_target_pairs={{0,2},{1,3},{2,0},{3,1},{4,6},{5,7},{6,4},{7,5},{8,10},{9,11},{10,... | collective-permute-start | bytes 1081352 | tf_op jit(solution)/shard_map/ppermute | solution.py:199
  60.1 16.1 %collective-permute-start.2 = (bf16[1408,128]{1,0:T(8,128)(2,1)S(1)}, bf16[1408,128]{1,0:T(8,128)(2,1)S(1)}, u32[]{:S(2)}, u32[]{:S(2)}) collective-permute-start(bf16[1408,128]{1,0:T(8,128)(2,1)S(1)} %slice_dynamic-update-slice_fusion.refs_0_), channel_id=1, source_target_pairs={{0,3},{1,0},{2,1},{3,2},{4,7},{5,4},{6,5},{7,6},{8,11},{9,8},{10,9... | collective-permute-start | bytes 1081352 | tf_op jit(solution)/shard_map/ppermute | solution.py:199

commit v2 on v1

--- a/solution.py
+++ b/solution.py
@@ -22,8 +22,7 @@
 GROUP = 128
 KEYS = 32
 UNIT = 2 * GROUP
-SPAN = 4
-CHUNK = SPAN * ZH * KEYS
+HALF = YS * ZH // 2
 PACKED = KEYS * (D_LATENT + ROPE) // 128
 VMEM_LIMIT = 20 * 2**20
 OUT_ROWS = 2 * VDIM + 16
@@ -56,58 +55,62 @@
             qcat_ref[512:768, cols] = jnp.concatenate([high, none, low, none], axis=0)
 
 
-def one_chunk(kv_ref, index, allowed, qcat_ref, m_ref, l_ref, acc_ref):
-    block = kv_ref[pl.ds(index * SPAN * ZH, SPAN * ZH)]
+def attend_groups(groups, kv_ref, key_zl, key_c, qcat_ref, old, new):
+    y, zh, zl, c, x = (lax.axis_index(a) for a in ("y", "zh", "zl", "c", "x"))
+    count, free = groups * KEYS, (groups - HALF) * KEYS
+    block = kv_ref[0:groups]
     latent = jnp.concatenate(
-        [block[:, 0:KEYS].reshape(CHUNK, 128), block[:, KEYS : 2 * KEYS].reshape(CHUNK, 128)], axis=1
+        [block[:, 0:KEYS].reshape(count, 128), block[:, KEYS : 2 * KEYS].reshape(count, 128)], axis=1
     )
     packed = block[:, 2 * KEYS :].astype(f32)
-    other = pltpu.roll(packed.reshape(CHUNK // 2, 128), 64, 1).reshape(packed.shape)
-    rope = jnp.concatenate([packed, other], axis=1).astype(bf16).reshape(CHUNK, 128)
+    other = pltpu.roll(packed.reshape(count // 2, 128), 64, 1).reshape(packed.shape)
+    rope = jnp.concatenate([packed, other], axis=1).astype(bf16).reshape(count, 128)
     keys = jnp.concatenate([latent, latent, rope, rope], axis=1)
     turned = latent.T
+    key = free + lax.broadcasted_iota(jnp.int32, (count - free, UNIT), 0)
+    row = lax.broadcasted_iota(jnp.int32, (count - free, UNIT), 1) % GROUP
+    query_pos = (((y * ZH + zh) * ZL + zl) * CS + c) * GROUP + row
+    key_pos = (((key // KEYS) * ZL + key_zl) * CS + key_c) * GROUP + x * KEYS + key % KEYS
+    allowed = key_pos <= query_pos
+    m_ref, l_ref, acc_ref = new
     units = [pl.ds(u * UNIT, UNIT) for u in range(XS)]
     scores = [jnp.dot(keys, qcat_ref[:, cols], preferred_element_type=f32) for cols in units]
     for s, cols in zip(scores, units):
-        if allowed is not None:
-            s = jnp.where(allowed, s, MASKED)
-        m_old = m_ref[:, cols]
-        m_new = jnp.maximum(m_old, jnp.max(s, axis=0, keepdims=True))
-        factor = jnp.exp2(m_old - m_new)
-        weights = jnp.exp2(s - m_new)
-        l_ref[:, cols] = l_ref[:, cols] * factor + jnp.sum(weights, axis=0, keepdims=True)
-        m_ref[:, cols] = m_new
+        masked = jnp.where(allowed, s[free:], MASKED)
+        s = jnp.concatenate([s[:free], masked], axis=0) if free else masked
+        top = jnp.max(s, axis=0, keepdims=True)
+        top = jnp.maximum(top, LOWEST if old is None else old[0][:, cols])
+        weights = jnp.exp2(s - top)
+        total = jnp.sum(weights, axis=0, keepdims=True)
         update = jnp.dot(turned, weights.astype(bf16), preferred_element_type=f32)
-        acc_ref[:, cols] = acc_ref[:, cols] * factor + update
-
-
-def attend(kv_ref, same_parity, same_core, qcat_ref, m_ref, l_ref, acc_ref):
-    y, zh, zl, c, x = (lax.axis_index(a) for a in ("y", "zh", "zl", "c", "x"))
+        if old is not None:
+            factor = jnp.exp2(old[0][:, cols] - top)
+            total = total + old[1][:, cols] * factor
+            update = update + old[2][:, cols] * factor
+        m_ref[:, cols], l_ref[:, cols], acc_ref[:, cols] = top, total, update
+
+
+def attend(same_parity, same_core, kv_ref, qcat_ref, old, new):
+    zl, c = lax.axis_index("zl"), lax.axis_index("c")
     key_zl = zl if same_parity else 1 - zl
     key_c = c if same_core else 1 - c
-    last = y // SPAN
-    key = lax.broadcasted_iota(jnp.int32, (CHUNK, UNIT), 0)
-    row = lax.broadcasted_iota(jnp.int32, (CHUNK, UNIT), 1) % GROUP
-    query_pos = (((y * ZH + zh) * ZL + zl) * CS + c) * GROUP + row
-    key_group = ((last * SPAN * ZH + key // KEYS) * ZL + key_zl) * CS + key_c
-    key_pos = key_group * GROUP + x * KEYS + key % KEYS
-    refs = (qcat_ref, m_ref, l_ref, acc_ref)
-    one_chunk(kv_ref, last, key_pos <= query_pos, *refs)
-    lax.fori_loop(0, last, lambda i, _: one_chunk(kv_ref, i, None, *refs), None)
+    upper = lax.axis_index("y") >= YS // 2
+
+    @pl.when(upper)
+    def _():
+        attend_groups(2 * HALF, kv_ref, key_zl, key_c, qcat_ref, old, new)
+
+    @pl.when(jnp.logical_not(upper))
+    def _():
+        attend_groups(HALF, kv_ref, key_zl, key_c, qcat_ref, old, new)
 
 
 def attend_first(kv_ref, qcat_ref, m_ref, l_ref, acc_ref):
-    m_ref[...] = jnp.full(m_ref.shape, LOWEST, f32)
-    l_ref[...] = jnp.zeros(l_ref.shape, f32)
-    acc_ref[...] = jnp.zeros(acc_ref.shape, f32)
-    attend(kv_ref, True, True, qcat_ref, m_ref, l_ref, acc_ref)
+    attend(True, True, kv_ref, qcat_ref, None, (m_ref, l_ref, acc_ref))
 
 
 def attend_more(same_parity, same_core, kv_ref, qcat_ref, m_in, l_in, acc_in, m_ref, l_ref, acc_ref):
-    m_ref[...] = m_in[...]
-    l_ref[...] = l_in[...]
-    acc_ref[...] = acc_in[...]
-    attend(kv_ref, same_parity, same_core, qcat_ref, m_ref, l_ref, acc_ref)
+    attend(same_parity, same_core, kv_ref, qcat_ref, (m_in, l_in, acc_in), (m_ref, l_ref, acc_ref))
 
 
 def thirds(value):

time: 102 us -> 101 us (level)
  Pallas kernels: 15.1 us -> 14 us
    pallas_call x7, Pallas kernels: 15.1 us -> 14 us  [call(): pl.pallas_call(kernel, out_shape=out_shape, in_specs=[pl.BlockSpec(memory...]
  transfers between devices with their start and end apart: 8 -> 8, of which waited for: 6 -> 6; matrix products, arithmetic and copies ran while one was open for 0% -> 0% of each run, Pallas kernels for 10% -> 9%
where the time goes in v2:
time: 101 us; the launch traced here: 100 us
  starting transfers between devices  38.1 us (38%)
  waiting for transfers between devices  36 us (36%)
  Pallas kernels  14 us (14%)
  blocking collectives  10.8 us (11%)
  local copies, waits for them, and re-layouts  1.11 us (1%)
    all_to_all x1, waiting for transfers between devices, steps(): lax.all_to_all(copies, ('y', 'zh'), split_axis=0, concat_axis=0, tiled=True)  19.2 us
    all_to_all x1, starting transfers between devices, steps(): lax.all_to_all(copies, ('y', 'zh'), split_axis=0, concat_axis=0, tiled=True)  15.8 us
    pallas_call x7, Pallas kernels, call(): pl.pallas_call(kernel, out_shape=out_shape, in_specs=[pl.BlockSpec(memory...  14 us
    ppermute x3, waiting for transfers between devices, steps(): lax.ppermute(own, 'x', [(i, (i + k) % XS) for i in range(XS)])  12.8 us
    ppermute x3, starting transfers between devices, steps(): lax.ppermute(own, 'x', [(i, (i + k) % XS) for i in range(XS)])  11.4 us
    all_to_all x1, blocking collectives, steps(): parts = lax.all_to_all(parts, 'x', split_axis=0, concat_axis=0, tiled=True)  10.8 us
    ppermute x1, starting transfers between devices, steps(): lax.ppermute(near[:middle], ('zh', 'zl'), [(i, (i + 1) % zs) for i in ran...  3.77 us
    ppermute x1, starting transfers between devices, steps(): lax.ppermute(near[middle:], ('zh', 'zl'), [(i, (i - 1) % zs) for i in ran...  3.28 us
  transfers between devices with their start and end apart: 8, of which 6 were waited for; matrix products, arithmetic and copies ran while one was open for 0% of the time, Pallas kernels for 9%

profile of v2, /device:TPU:48, one launch (start us, length us, event | category | flops | bytes accessed | tf_op | source)
XLA Modules:
  0.0 100.3 jit_solution(6678638478893726497)
XLA Ops:
  0.0 0.7 copy-done
  0.7 0.9 shard_map.38
  1.7 15.8 %all-to-all-start = ((bf16[32,80,128]{2,1,0:T(8,128)(2,1)}), bf16[32,80,128]{2,1,0:T(8,128)(2,1)S(1)}, u32[]{:S(2)}, u32[]{:S(2)}) async-start(bf16[32,80,128]{2,1,0:T(8,128)(2,1)} %shard_map.38), calls=%async_computation | async-start | bytes 1310720 | tf_op jit(solution)/shard_map/all_to_all | solution.py:193
  17.7 0.1 maximum_dynamic-update-slice_fusion
  17.7 19.2 %all-to-all-done.kv_ref = bf16[32,80,128]{2,1,0:T(8,128)(2,1)S(1)} async-done(((bf16[32,80,128]{2,1,0:T(8,128)(2,1)}), bf16[32,80,128]{2,1,0:T(8,128)(2,1)S(1)}, u32[]{:S(2)}, u32[]{:S(2)}) %all-to-all-start) | async-done | bytes 655392 | tf_op jit(solution)/shard_map/all_to_all | solution.py:193
  37.0 3.8 %collective-permute-start.3 = (bf16[16,80,128]{2,1,0:T(8,128)(2,1)S(1)}, bf16[16,80,128]{2,1,0:T(8,128)(2,1)S(1)}, u32[]{:S(2)}, u32[]{:S(2)}) collective-permute-start(bf16[16,80,128]{2,1,0:T(8,128)(2,1)S(1)} %get-tuple-element.28), channel_id=1, source_target_pairs={{0,8},{8,16},{16,24},{24,32},{32,40},{40,48},{48,56},{56,0},{1,9},... | collective-permute-start | bytes 983048 | tf_op jit(solution)/shard_map/ppermute | solution.py:210
  40.8 3.3 %collective-permute-start.4 = (bf16[16,80,128]{2,1,0:T(8,128)(2,1)S(1)}, bf16[16,80,128]{2,1,0:T(8,128)(2,1)S(1)}, u32[]{:S(2)}, u32[]{:S(2)}) collective-permute-start(bf16[16,80,128]{2,1,0:T(8,128)(2,1)S(1)} %get-tuple-element.27), channel_id=1, source_target_pairs={{0,56},{8,0},{16,8},{24,16},{32,24},{40,32},{48,40},{56,48},{1,57}... | collective-permute-start | bytes 983048 | tf_op jit(solution)/shard_map/ppermute | solution.py:211
  44.1 1.9 %collective-permute-start.6 = (bf16[32,80,128]{2,1,0:T(8,128)(2,1)S(1)}, bf16[32,80,128]{2,1,0:T(8,128)(2,1)S(1)}, u32[]{:S(2)}, u32[]{:S(2)}) collective-permute-start(bf16[32,80,128]{2,1,0:T(8,128)(2,1)S(1)} %all-to-all-done.kv_ref), channel_id=1, source_target_pairs={{0,4},{4,0},{1,5},{5,1},{2,6},{6,2},{3,7},{7,3},{8,12},{12,8},{9,1... | collective-permute-start | bytes 1966088 | tf_op jit(solution)/shard_map/ppermute | solution.py:213
  46.1 2.2 %collective-permute-done.3 = bf16[16,80,128]{2,1,0:T(8,128)(2,1)S(1)} collective-permute-done((bf16[16,80,128]{2,1,0:T(8,128)(2,1)S(1)}, bf16[16,80,128]{2,1,0:T(8,128)(2,1)S(1)}, u32[]{:S(2)}, u32[]{:S(2)}) %collective-permute-start.3) | collective-permute-done | bytes 327712 | tf_op jit(solution)/shard_map/ppermute | solution.py:210
  48.2 1.8 %collective-permute-done.4 = bf16[16,80,128]{2,1,0:T(8,128)(2,1)S(1)} collective-permute-done((bf16[16,80,128]{2,1,0:T(8,128)(2,1)S(1)}, bf16[16,80,128]{2,1,0:T(8,128)(2,1)S(1)}, u32[]{:S(2)}, u32[]{:S(2)}) %collective-permute-start.4) | collective-permute-done | bytes 327712 | tf_op jit(solution)/shard_map/ppermute | solution.py:211
  50.1 1.9 %collective-permute-start.5 = (bf16[32,80,128]{2,1,0:T(8,128)(2,1)S(1)}, bf16[32,80,128]{2,1,0:T(8,128)(2,1)S(1)}, u32[]{:S(2)}, u32[]{:S(2)}) collective-permute-start(bf16[32,80,128]{2,1,0:T(8,128)(2,1)S(1)} %constant_dynamic-update-slice_fusion.kv_ref), channel_id=1, source_target_pairs={{0,4},{4,0},{1,5},{5,1},{2,6},{6,2},{3,7},{7,3},{8,12},{12,8},{9,1... | collective-permute-start | bytes 1966088 | tf_op jit(solution)/shard_map/ppermute | solution.py:217
  52.1 3.4 %collective-permute-start = (bf16[1408,128]{1,0:T(8,128)(2,1)S(1)}, bf16[1408,128]{1,0:T(8,128)(2,1)S(1)}, u32[]{:S(2)}, u32[]{:S(2)}) collective-permute-start(bf16[1408,128]{1,0:T(8,128)(2,1)S(1)} %slice_dynamic-update-slice_fusion.refs_0_), channel_id=1, source_target_pairs={{0,1},{1,2},{2,3},{3,0},{4,5},{5,6},{6,7},{7,4},{8,9},{9,10},{10,1... | collective-permute-start | bytes 1081352 | tf_op jit(solution)/shard_map/ppermute | solution.py:202
  55.5 4.6 %collective-permute-start.1 = (bf16[1408,128]{1,0:T(8,128)(2,1)S(1)}, bf16[1408,128]{1,0:T(8,128)(2,1)S(1)}, u32[]{:S(2)}, u32[]{:S(2)}) collective-permute-start(bf16[1408,128]{1,0:T(8,128)(2,1)S(1)} %slice_dynamic-update-slice_fusion.refs_0_), channel_id=1, source_target_pairs={{0,2},{1,3},{2,0},{3,1},{4,6},{5,7},{6,4},{7,5},{8,10},{9,11},{10,... | collective-permute-start | bytes 1081352 | tf_op jit(solution)/shard_map/ppermute | solution.py:202
  60.1 3.3 %collective-permute-start.2 = (bf16[1408,128]{1,0:T(8,128)(2,1)S(1)}, bf16[1408,128]{1,0:T(8,128)(2,1)S(1)}, u32[]{:S(2)}, u32[]{:S(2)}) collective-permute-start(bf16[1408,128]{1,0:T(8,128)(2,1)S(1)} %slice_dynamic-update-slice_fusion.refs_0_), channel_id=1, source_target_pairs={{0,3},{1,0},{2,1},{3,2},{4,7},{5,4},{6,5},{7,6},{8,11},{9,8},{10,9... | collective-permute-start | bytes 1081352 | tf_op jit(solution)/shard_map/ppermute | solution.py:202
  63.5 2.5 %collective-permute-done.refs_1_ = bf16[1408,128]{1,0:T(8,128)(2,1)S(1)} collective-permute-done((bf16[1408,128]{1,0:T(8,128)(2,1)S(1)}, bf16[1408,128]{1,0:T(8,128)(2,1)S(1)}, u32[]{:S(2)}, u32[]{:S(2)}) %collective-permute-start) | collective-permute-done | bytes 360480 | tf_op jit(solution)/shard_map/ppermute | solution.py:202
  66.0 8.7 %collective-permute-done.1.refs_2_ = bf16[1408,128]{1,0:T(8,128)(2,1)S(1)} collective-permute-done((bf16[1408,128]{1,0:T(8,128)(2,1)S(1)}, bf16[1408,128]{1,0:T(8,128)(2,1)S(1)}, u32[]{:S(2)}, u32[]{:S(2)}) %collective-permute-start.1) | collective-permute-done | bytes 360480 | tf_op jit(solution)/shard_map/ppermute | solution.py:202
  74.7 1.6 %collective-permute-done.2.refs_3_ = bf16[1408,128]{1,0:T(8,128)(2,1)S(1)} collective-permute-done((bf16[1408,128]{1,0:T(8,128)(2,1)S(1)}, bf16[1408,128]{1,0:T(8,128)(2,1)S(1)}, u32[]{:S(2)}, u32[]{:S(2)}) %collective-permute-start.2) | collective-permute-done | bytes 360480 | tf_op jit(solution)/shard_map/ppermute | solution.py:202
  76.3 0.4 shard_map.37
  76.7 2.8 %shard_map.39 = (f32[1,1024]{1,0:T(1,128)S(1)}, f32[1,1024]{1,0:T(1,128)S(1)}, f32[256,1024]{1,0:T(8,128)S(1)}) custom-call(bf16[32,80,128]{2,1,0:T(8,128)(2,1)S(1)} %all-to-all-done.kv_ref, bf16[768,1024]{1,0:T(8,128)(2,1)S(1)} %get-tuple-element.17.qcat_ref), custom_call_target="tpu_custom_call" | custom-call | tf_op jit(solution)/shard_map/pallas_call | solution.py:159
  79.5 2.8 %shard_map.40 = (f32[1,1024]{1,0:T(1,128)S(1)}, f32[1,1024]{1,0:T(1,128)S(1)}, f32[256,1024]{1,0:T(8,128)S(1)}) custom-call(bf16[32,80,128]{2,1,0:T(8,128)(2,1)S(1)} %collective-permute-done.6.kv_ref, bf16[768,1024]{1,0:T(8,128)(2,1)S(1)} %get-tuple-element.17.qcat_ref, f32[1,1024]{1,0:T(1,128)S(1)} %get-tuple-element.18.m_in, ...), custom_call_target="tpu_custom_call" | custom-call | tf_op jit(solution)/shard_map/pallas_call | solution.py:159
  82.4 3.0 %shard_map.41 = (f32[1,1024]{1,0:T(1,128)S(1)}, f32[1,1024]{1,0:T(1,128)S(1)}, f32[256,1024]{1,0:T(8,128)S(1)}) custom-call(bf16[32,80,128]{2,1,0:T(8,128)(2,1)S(1)} %constant_dynamic-update-slice_fusion.kv_ref, bf16[768,1024]{1,0:T(8,128)(2,1)S(1)} %get-tuple-element.17.qcat_ref, f32[1,1024]{1,0:T(1,128)S(1)} %get-tuple-element.21.m_in, ...), custom_call_target="tpu_custom_call" | custom-call | tf_op jit(solution)/shard_map/pallas_call | solution.py:159
  85.4 3.3 %shard_map.42 = bf16[4,272,128]{2,1,0:T(8,128)(2,1)S(1)} custom-call(bf16[8,128,256]{2,1,0:T(8,128)(2,1)S(1)} %get-tuple-element.16.values_ref, bf16[32,80,128]{2,1,0:T(8,128)(2,1)S(1)} %collective-permute-done.5.kv_ref, bf16[768,1024]{1,0:T(8,128)(2,1)S(1)} %get-tuple-element.17.qcat_ref, f32[1,1024]{1,0:T(1,128)S(1)} %get-tuple-element.24.m_in, ...), custom_call_target="tpu_custom_call" | custom-call | tf_op jit(solution)/shard_map/pallas_call | solution.py:159
  88.7 10.8 %all_to_all.10.parts_ref = bf16[4,272,128]{2,1,0:T(8,128)(2,1)S(1)} all-to-all(bf16[4,272,128]{2,1,0:T(8,128)(2,1)S(1)} %shard_map.42), channel_id=1, replica_groups=mesh['y'=8,'zh'=4,'zl'=2,'c'=2,'x'=4] {'x'}, dimensions={0} | all-to-all | bytes 557056 | tf_op jit(solution)/shard_map/all_to_all | solution.py:225
  99.5 0.8 shard_map.43
  (17 shorter events, 0.4 us)
Async XLA Ops:
  0.0 0.7 copy-start
  0.7 16.7 %copy-start.2 = (bf16[128,384]{1,0:T(8,128)(2,1)S(1)}, bf16[128,384]{1,0:T(8,128)(2,1)}, u32[]{:S(2)}) copy-start(bf16[128,384]{1,0:T(8,128)(2,1)} %param.3) | copy-start | bytes 294916
  1.7 39.1 %copy-start.1 = (bf16[256,512]{1,0:T(8,128)(2,1)S(1)}, bf16[256,512]{1,0:T(8,128)(2,1)}, u32[]{:S(2)}) copy-start(bf16[256,512]{1,0:T(8,128)(2,1)} %param.5) | copy-start | bytes 786436
  1.7 35.3 %all-to-all-start = ((bf16[32,80,128]{2,1,0:T(8,128)(2,1)}), bf16[32,80,128]{2,1,0:T(8,128)(2,1)S(1)}, u32[]{:S(2)}, u32[]{:S(2)}) async-start(bf16[32,80,128]{2,1,0:T(8,128)(2,1)} %shard_map.38), calls=%async_computation | async-start | bytes 1310720 | tf_op jit(solution)/shard_map/all_to_all | solution.py:193
  37.0 11.2 %collective-permute-start.3 = (bf16[16,80,128]{2,1,0:T(8,128)(2,1)S(1)}, bf16[16,80,128]{2,1,0:T(8,128)(2,1)S(1)}, u32[]{:S(2)}, u32[]{:S(2)}) collective-permute-start(bf16[16,80,128]{2,1,0:T(8,128)(2,1)S(1)} %get-tuple-element.28), channel_id=1, source_target_pairs={{0,8},{8,16},{16,24},{24,32},{32,40},{40,48},{48,56},{56,0},{1,9},... | collective-permute-start | bytes 983048 | tf_op jit(solution)/shard_map/ppermute | solution.py:210
  40.8 9.3 %collective-permute-start.4 = (bf16[16,80,128]{2,1,0:T(8,128)(2,1)S(1)}, bf16[16,80,128]{2,1,0:T(8,128)(2,1)S(1)}, u32[]{:S(2)}, u32[]{:S(2)}) collective-permute-start(bf16[16,80,128]{2,1,0:T(8,128)(2,1)S(1)} %get-tuple-element.27), channel_id=1, source_target_pairs={{0,56},{8,0},{16,8},{24,16},{32,24},{40,32},{48,40},{56,48},{1,57}... | collective-permute-start | bytes 983048 | tf_op jit(solution)/shard_map/ppermute | solution.py:211
  44.1 35.4 %collective-permute-start.6 = (bf16[32,80,128]{2,1,0:T(8,128)(2,1)S(1)}, bf16[32,80,128]{2,1,0:T(8,128)(2,1)S(1)}, u32[]{:S(2)}, u32[]{:S(2)}) collective-permute-start(bf16[32,80,128]{2,1,0:T(8,128)(2,1)S(1)} %all-to-all-done.kv_ref), channel_id=1, source_target_pairs={{0,4},{4,0},{1,5},{5,1},{2,6},{6,2},{3,7},{7,3},{8,12},{12,8},{9,1... | collective-permute-start | bytes 1966088 | tf_op jit(solution)/shard_map/ppermute | solution.py:213
  50.1 35.3 %collective-permute-start.5 = (bf16[32,80,128]{2,1,0:T(8,128)(2,1)S(1)}, bf16[32,80,128]{2,1,0:T(8,128)(2,1)S(1)}, u32[]{:S(2)}, u32[]{:S(2)}) collective-permute-start(bf16[32,80,128]{2,1,0:T(8,128)(2,1)S(1)} %constant_dynamic-update-slice_fusion.kv_ref), channel_id=1, source_target_pairs={{0,4},{4,0},{1,5},{5,1},{2,6},{6,2},{3,7},{7,3},{8,12},{12,8},{9,1... | collective-permute-start | bytes 1966088 | tf_op jit(solution)/shard_map/ppermute | solution.py:217
  52.1 13.9 %collective-permute-start = (bf16[1408,128]{1,0:T(8,128)(2,1)S(1)}, bf16[1408,128]{1,0:T(8,128)(2,1)S(1)}, u32[]{:S(2)}, u32[]{:S(2)}) collective-permute-start(bf16[1408,128]{1,0:T(8,128)(2,1)S(1)} %slice_dynamic-update-slice_fusion.refs_0_), channel_id=1, source_target_pairs={{0,1},{1,2},{2,3},{3,0},{4,5},{5,6},{6,7},{7,4},{8,9},{9,10},{10,1... | collective-permute-start | bytes 1081352 | tf_op jit(solution)/shard_map/ppermute | solution.py:202
  55.5 19.2 %collective-permute-start.1 = (bf16[1408,128]{1,0:T(8,128)(2,1)S(1)}, bf16[1408,128]{1,0:T(8,128)(2,1)S(1)}, u32[]{:S(2)}, u32[]{:S(2)}) collective-permute-start(bf16[1408,128]{1,0:T(8,128)(2,1)S(1)} %slice_dynamic-update-slice_fusion.refs_0_), channel_id=1, source_target_pairs={{0,2},{1,3},{2,0},{3,1},{4,6},{5,7},{6,4},{7,5},{8,10},{9,11},{10,... | collective-permute-start | bytes 1081352 | tf_op jit(solution)/shard_map/ppermute | solution.py:202
  60.1 16.1 %collective-permute-start.2 = (bf16[1408,128]{1,0:T(8,128)(2,1)S(1)}, bf16[1408,128]{1,0:T(8,128)(2,1)S(1)}, u32[]{:S(2)}, u32[]{:S(2)}) collective-permute-start(bf16[1408,128]{1,0:T(8,128)(2,1)S(1)} %slice_dynamic-update-slice_fusion.refs_0_), channel_id=1, source_target_pairs={{0,3},{1,0},{2,1},{3,2},{4,7},{5,4},{6,5},{7,6},{8,11},{9,8},{10,9... | collective-permute-start | bytes 1081352 | tf_op jit(solution)/shard_map/ppermute | solution.py:202

commit v3 on v2

--- a/solution.py
+++ b/solution.py
@@ -206,14 +206,15 @@
         jax.ShapeDtypeStruct((2 * XS, VDIM, D_LATENT), bf16),
     )
     qcat, values = call(query_kernel, shapes, *qws)
-    zs, middle = ZH * ZL, YS * ZH // 2
-    low = lax.ppermute(near[:middle], ("zh", "zl"), [(i, (i + 1) % zs) for i in range(zs)])
-    high = lax.ppermute(near[middle:], ("zh", "zl"), [(i, (i - 1) % zs) for i in range(zs)])
+    zs = ZH * ZL
+    up = [((z, 1), ((z + 1) % zs, 1)) for z in range(zs)]
+    down = [((z, 0), ((z - 1) % zs, 0)) for z in range(zs)]
+    pairs = [(z * CS + c, to_z * CS + to_c) for (z, c), (to_z, to_c) in up + down]
+    far = lax.ppermute(near, ("zh", "zl", "c"), pairs)
     swap = [(0, 1), (1, 0)]
     near_other = lax.ppermute(near, "c", swap)
     m, l, acc = call(attend_first, state, near, qcat)
     m, l, acc = call(functools.partial(attend_more, True, False), state, near_other, qcat, m, l, acc)
-    far = jnp.concatenate([low, high])
     far_other = lax.ppermute(far, "c", swap)
     m, l, acc = call(functools.partial(attend_more, False, True), state, far, qcat, m, l, acc)
     parts = call(

time: 101 us -> 100 us (0.990)
  the two profiles are of different devices: /device:TPU:48 before, /device:TPU:40 now
where the time goes in v3:
time: 100 us; the launch traced here: 99.8 us
  waiting for transfers between devices  40 us (40%)
  starting transfers between devices  33.7 us (34%)
  Pallas kernels  14 us (14%)
  blocking collectives  10.9 us (11%)
  local copies, waits for them, and re-layouts  1 us (1%)
    all_to_all x1, waiting for transfers between devices, steps(): lax.all_to_all(copies, ('y', 'zh'), split_axis=0, concat_axis=0, tiled=True)  19.6 us
    all_to_all x1, starting transfers between devices, steps(): lax.all_to_all(copies, ('y', 'zh'), split_axis=0, concat_axis=0, tiled=True)  15.7 us
    pallas_call x7, Pallas kernels, call(): pl.pallas_call(kernel, out_shape=out_shape, in_specs=[pl.BlockSpec(memory...  14 us
    ppermute x3, waiting for transfers between devices, steps(): lax.ppermute(own, 'x', [(i, (i + k) % XS) for i in range(XS)])  12.8 us
    ppermute x3, starting transfers between devices, steps(): lax.ppermute(own, 'x', [(i, (i + k) % XS) for i in range(XS)])  11.4 us
    all_to_all x1, blocking collectives, steps(): parts = lax.all_to_all(parts, 'x', split_axis=0, concat_axis=0, tiled=True)  10.9 us
    ppermute x1, waiting for transfers between devices, steps(): far = lax.ppermute(near, ('zh', 'zl', 'c'), pairs)  7.57 us
    ppermute x1, starting transfers between devices, steps(): far = lax.ppermute(near, ('zh', 'zl', 'c'), pairs)  2.72 us
  transfers between devices with their start and end apart: 7, of which 5 were waited for; matrix products, arithmetic and copies ran while one was open for 0% of the time, Pallas kernels for 9%

profile of v3, /device:TPU:40, one launch (start us, length us, event | category | flops | bytes accessed | tf_op | source)
XLA Modules:
  0.0 99.8 jit_solution(13828840773564252019)
XLA Ops:
  0.0 0.7 copy-done
  0.7 0.9 shard_map.38
  1.7 15.7 %all-to-all-start = ((bf16[32,80,128]{2,1,0:T(8,128)(2,1)}), bf16[32,80,128]{2,1,0:T(8,128)(2,1)S(1)}, u32[]{:S(2)}, u32[]{:S(2)}) async-start(bf16[32,80,128]{2,1,0:T(8,128)(2,1)} %shard_map.38), calls=%async_computation | async-start | bytes 1310720 | tf_op jit(solution)/shard_map/all_to_all | solution.py:193
  17.4 0.1 fusion
  17.5 19.6 %all-to-all-done.kv_ref = bf16[32,80,128]{2,1,0:T(8,128)(2,1)S(1)} async-done(((bf16[32,80,128]{2,1,0:T(8,128)(2,1)}), bf16[32,80,128]{2,1,0:T(8,128)(2,1)S(1)}, u32[]{:S(2)}, u32[]{:S(2)}) %all-to-all-start) | async-done | bytes 655392 | tf_op jit(solution)/shard_map/all_to_all | solution.py:193
  37.1 2.7 %collective-permute-start.3 = (bf16[32,80,128]{2,1,0:T(8,128)(2,1)S(1)}, bf16[32,80,128]{2,1,0:T(8,128)(2,1)S(1)}, u32[]{:S(2)}, u32[]{:S(2)}) collective-permute-start(bf16[32,80,128]{2,1,0:T(8,128)(2,1)S(1)} %all-to-all-done.kv_ref), channel_id=1, source_target_pairs={{4,12},{12,20},{20,28},{28,36},{36,44},{44,52},{52,60},{60,4},{0,5... | collective-permute-start | bytes 1966088 | tf_op jit(solution)/shard_map/ppermute | solution.py:213
  39.9 0.1 slice_dynamic-update-slice_fusion.4
  40.0 0.1 maximum_dynamic-update-slice_fusion
  40.1 1.9 %collective-permute-start.5 = (bf16[32,80,128]{2,1,0:T(8,128)(2,1)S(1)}, bf16[32,80,128]{2,1,0:T(8,128)(2,1)S(1)}, u32[]{:S(2)}, u32[]{:S(2)}) collective-permute-start(bf16[32,80,128]{2,1,0:T(8,128)(2,1)S(1)} %all-to-all-done.kv_ref), channel_id=1, source_target_pairs={{0,4},{4,0},{1,5},{5,1},{2,6},{6,2},{3,7},{7,3},{8,12},{12,8},{9,1... | collective-permute-start | bytes 1966088 | tf_op jit(solution)/shard_map/ppermute | solution.py:215
  42.0 7.6 %collective-permute-done.3.kv_ref = bf16[32,80,128]{2,1,0:T(8,128)(2,1)S(1)} collective-permute-done((bf16[32,80,128]{2,1,0:T(8,128)(2,1)S(1)}, bf16[32,80,128]{2,1,0:T(8,128)(2,1)S(1)}, u32[]{:S(2)}, u32[]{:S(2)}) %collective-permute-start.3) | collective-permute-done | bytes 655392 | tf_op jit(solution)/shard_map/ppermute | solution.py:213
  49.6 1.9 %collective-permute-start.4 = (bf16[32,80,128]{2,1,0:T(8,128)(2,1)S(1)}, bf16[32,80,128]{2,1,0:T(8,128)(2,1)S(1)}, u32[]{:S(2)}, u32[]{:S(2)}) collective-permute-start(bf16[32,80,128]{2,1,0:T(8,128)(2,1)S(1)} %collective-permute-done.3.kv_ref), channel_id=1, source_target_pairs={{0,4},{4,0},{1,5},{5,1},{2,6},{6,2},{3,7},{7,3},{8,12},{12,8},{9,1... | collective-permute-start | bytes 1966088 | tf_op jit(solution)/shard_map/ppermute | solution.py:218
  51.6 3.4 %collective-permute-start = (bf16[1408,128]{1,0:T(8,128)(2,1)S(1)}, bf16[1408,128]{1,0:T(8,128)(2,1)S(1)}, u32[]{:S(2)}, u32[]{:S(2)}) collective-permute-start(bf16[1408,128]{1,0:T(8,128)(2,1)S(1)} %slice_dynamic-update-slice_fusion.refs_0_), channel_id=1, source_target_pairs={{0,1},{1,2},{2,3},{3,0},{4,5},{5,6},{6,7},{7,4},{8,9},{9,10},{10,1... | collective-permute-start | bytes 1081352 | tf_op jit(solution)/shard_map/ppermute | solution.py:202
  55.0 4.6 %collective-permute-start.1 = (bf16[1408,128]{1,0:T(8,128)(2,1)S(1)}, bf16[1408,128]{1,0:T(8,128)(2,1)S(1)}, u32[]{:S(2)}, u32[]{:S(2)}) collective-permute-start(bf16[1408,128]{1,0:T(8,128)(2,1)S(1)} %slice_dynamic-update-slice_fusion.refs_0_), channel_id=1, source_target_pairs={{0,2},{1,3},{2,0},{3,1},{4,6},{5,7},{6,4},{7,5},{8,10},{9,11},{10,... | collective-permute-start | bytes 1081352 | tf_op jit(solution)/shard_map/ppermute | solution.py:202
  59.6 3.3 %collective-permute-start.2 = (bf16[1408,128]{1,0:T(8,128)(2,1)S(1)}, bf16[1408,128]{1,0:T(8,128)(2,1)S(1)}, u32[]{:S(2)}, u32[]{:S(2)}) collective-permute-start(bf16[1408,128]{1,0:T(8,128)(2,1)S(1)} %slice_dynamic-update-slice_fusion.refs_0_), channel_id=1, source_target_pairs={{0,3},{1,0},{2,1},{3,2},{4,7},{5,4},{6,5},{7,6},{8,11},{9,8},{10,9... | collective-permute-start | bytes 1081352 | tf_op jit(solution)/shard_map/ppermute | solution.py:202
  63.0 2.5 %collective-permute-done.refs_1_ = bf16[1408,128]{1,0:T(8,128)(2,1)S(1)} collective-permute-done((bf16[1408,128]{1,0:T(8,128)(2,1)S(1)}, bf16[1408,128]{1,0:T(8,128)(2,1)S(1)}, u32[]{:S(2)}, u32[]{:S(2)}) %collective-permute-start) | collective-permute-done | bytes 360480 | tf_op jit(solution)/shard_map/ppermute | solution.py:202
  65.5 8.7 %collective-permute-done.1.refs_2_ = bf16[1408,128]{1,0:T(8,128)(2,1)S(1)} collective-permute-done((bf16[1408,128]{1,0:T(8,128)(2,1)S(1)}, bf16[1408,128]{1,0:T(8,128)(2,1)S(1)}, u32[]{:S(2)}, u32[]{:S(2)}) %collective-permute-start.1) | collective-permute-done | bytes 360480 | tf_op jit(solution)/shard_map/ppermute | solution.py:202
  74.2 1.6 %collective-permute-done.2.refs_3_ = bf16[1408,128]{1,0:T(8,128)(2,1)S(1)} collective-permute-done((bf16[1408,128]{1,0:T(8,128)(2,1)S(1)}, bf16[1408,128]{1,0:T(8,128)(2,1)S(1)}, u32[]{:S(2)}, u32[]{:S(2)}) %collective-permute-start.2) | collective-permute-done | bytes 360480 | tf_op jit(solution)/shard_map/ppermute | solution.py:202
  75.8 0.4 shard_map.37
  76.2 2.8 %shard_map.39 = (f32[1,1024]{1,0:T(1,128)S(1)}, f32[1,1024]{1,0:T(1,128)S(1)}, f32[256,1024]{1,0:T(8,128)S(1)}) custom-call(bf16[32,80,128]{2,1,0:T(8,128)(2,1)S(1)} %all-to-all-done.kv_ref, bf16[768,1024]{1,0:T(8,128)(2,1)S(1)} %get-tuple-element.17.qcat_ref), custom_call_target="tpu_custom_call" | custom-call | tf_op jit(solution)/shard_map/pallas_call | solution.py:159
  79.0 2.8 %shard_map.40 = (f32[1,1024]{1,0:T(1,128)S(1)}, f32[1,1024]{1,0:T(1,128)S(1)}, f32[256,1024]{1,0:T(8,128)S(1)}) custom-call(bf16[32,80,128]{2,1,0:T(8,128)(2,1)S(1)} %collective-permute-done.5.kv_ref, bf16[768,1024]{1,0:T(8,128)(2,1)S(1)} %get-tuple-element.17.qcat_ref, f32[1,1024]{1,0:T(1,128)S(1)} %get-tuple-element.18.m_in, ...), custom_call_target="tpu_custom_call" | custom-call | tf_op jit(solution)/shard_map/pallas_call | solution.py:159
  81.8 2.8 %shard_map.41 = (f32[1,1024]{1,0:T(1,128)S(1)}, f32[1,1024]{1,0:T(1,128)S(1)}, f32[256,1024]{1,0:T(8,128)S(1)}) custom-call(bf16[32,80,128]{2,1,0:T(8,128)(2,1)S(1)} %collective-permute-done.3.kv_ref, bf16[768,1024]{1,0:T(8,128)(2,1)S(1)} %get-tuple-element.17.qcat_ref, f32[1,1024]{1,0:T(1,128)S(1)} %get-tuple-element.21.m_in, ...), custom_call_target="tpu_custom_call" | custom-call | tf_op jit(solution)/shard_map/pallas_call | solution.py:159
  84.7 3.4 %shard_map.42 = bf16[4,272,128]{2,1,0:T(8,128)(2,1)S(1)} custom-call(bf16[8,128,256]{2,1,0:T(8,128)(2,1)S(1)} %get-tuple-element.16.values_ref, bf16[32,80,128]{2,1,0:T(8,128)(2,1)S(1)} %collective-permute-done.4.kv_ref, bf16[768,1024]{1,0:T(8,128)(2,1)S(1)} %get-tuple-element.17.qcat_ref, f32[1,1024]{1,0:T(1,128)S(1)} %get-tuple-element.24.m_in, ...), custom_call_target="tpu_custom_call" | custom-call | tf_op jit(solution)/shard_map/pallas_call | solution.py:159
  88.1 10.9 %all_to_all.10.parts_ref = bf16[4,272,128]{2,1,0:T(8,128)(2,1)S(1)} all-to-all(bf16[4,272,128]{2,1,0:T(8,128)(2,1)S(1)} %shard_map.42), channel_id=1, replica_groups=mesh['y'=8,'zh'=4,'zl'=2,'c'=2,'x'=4] {'x'}, dimensions={0} | all-to-all | bytes 557056 | tf_op jit(solution)/shard_map/all_to_all | solution.py:226
  99.0 0.8 shard_map.43
  (12 shorter events, 0.1 us)
Async XLA Ops:
  0.0 0.7 copy-start
  0.7 16.7 %copy-start.2 = (bf16[128,384]{1,0:T(8,128)(2,1)S(1)}, bf16[128,384]{1,0:T(8,128)(2,1)}, u32[]{:S(2)}) copy-start(bf16[128,384]{1,0:T(8,128)(2,1)} %param.3) | copy-start | bytes 294916
  0.7 39.3 %copy-start.1 = (bf16[256,512]{1,0:T(8,128)(2,1)S(1)}, bf16[256,512]{1,0:T(8,128)(2,1)}, u32[]{:S(2)}) copy-start(bf16[256,512]{1,0:T(8,128)(2,1)} %param.5) | copy-start | bytes 786436
  1.7 35.5 %all-to-all-start = ((bf16[32,80,128]{2,1,0:T(8,128)(2,1)}), bf16[32,80,128]{2,1,0:T(8,128)(2,1)S(1)}, u32[]{:S(2)}, u32[]{:S(2)}) async-start(bf16[32,80,128]{2,1,0:T(8,128)(2,1)} %shard_map.38), calls=%async_computation | async-start | bytes 1310720 | tf_op jit(solution)/shard_map/all_to_all | solution.py:193
  37.1 12.5 %collective-permute-start.3 = (bf16[32,80,128]{2,1,0:T(8,128)(2,1)S(1)}, bf16[32,80,128]{2,1,0:T(8,128)(2,1)S(1)}, u32[]{:S(2)}, u32[]{:S(2)}) collective-permute-start(bf16[32,80,128]{2,1,0:T(8,128)(2,1)S(1)} %all-to-all-done.kv_ref), channel_id=1, source_target_pairs={{4,12},{12,20},{20,28},{28,36},{36,44},{44,52},{52,60},{60,4},{0,5... | collective-permute-start | bytes 1966088 | tf_op jit(solution)/shard_map/ppermute | solution.py:213
  40.1 38.9 %collective-permute-start.5 = (bf16[32,80,128]{2,1,0:T(8,128)(2,1)S(1)}, bf16[32,80,128]{2,1,0:T(8,128)(2,1)S(1)}, u32[]{:S(2)}, u32[]{:S(2)}) collective-permute-start(bf16[32,80,128]{2,1,0:T(8,128)(2,1)S(1)} %all-to-all-done.kv_ref), channel_id=1, source_target_pairs={{0,4},{4,0},{1,5},{5,1},{2,6},{6,2},{3,7},{7,3},{8,12},{12,8},{9,1... | collective-permute-start | bytes 1966088 | tf_op jit(solution)/shard_map/ppermute | solution.py:215
  49.6 35.1 %collective-permute-start.4 = (bf16[32,80,128]{2,1,0:T(8,128)(2,1)S(1)}, bf16[32,80,128]{2,1,0:T(8,128)(2,1)S(1)}, u32[]{:S(2)}, u32[]{:S(2)}) collective-permute-start(bf16[32,80,128]{2,1,0:T(8,128)(2,1)S(1)} %collective-permute-done.3.kv_ref), channel_id=1, source_target_pairs={{0,4},{4,0},{1,5},{5,1},{2,6},{6,2},{3,7},{7,3},{8,12},{12,8},{9,1... | collective-permute-start | bytes 1966088 | tf_op jit(solution)/shard_map/ppermute | solution.py:218
  51.6 13.9 %collective-permute-start = (bf16[1408,128]{1,0:T(8,128)(2,1)S(1)}, bf16[1408,128]{1,0:T(8,128)(2,1)S(1)}, u32[]{:S(2)}, u32[]{:S(2)}) collective-permute-start(bf16[1408,128]{1,0:T(8,128)(2,1)S(1)} %slice_dynamic-update-slice_fusion.refs_0_), channel_id=1, source_target_pairs={{0,1},{1,2},{2,3},{3,0},{4,5},{5,6},{6,7},{7,4},{8,9},{9,10},{10,1... | collective-permute-start | bytes 1081352 | tf_op jit(solution)/shard_map/ppermute | solution.py:202
  55.0 19.2 %collective-permute-start.1 = (bf16[1408,128]{1,0:T(8,128)(2,1)S(1)}, bf16[1408,128]{1,0:T(8,128)(2,1)S(1)}, u32[]{:S(2)}, u32[]{:S(2)}) collective-permute-start(bf16[1408,128]{1,0:T(8,128)(2,1)S(1)} %slice_dynamic-update-slice_fusion.refs_0_), channel_id=1, source_target_pairs={{0,2},{1,3},{2,0},{3,1},{4,6},{5,7},{6,4},{7,5},{8,10},{9,11},{10,... | collective-permute-start | bytes 1081352 | tf_op jit(solution)/shard_map/ppermute | solution.py:202
  59.6 16.1 %collective-permute-start.2 = (bf16[1408,128]{1,0:T(8,128)(2,1)S(1)}, bf16[1408,128]{1,0:T(8,128)(2,1)S(1)}, u32[]{:S(2)}, u32[]{:S(2)}) collective-permute-start(bf16[1408,128]{1,0:T(8,128)(2,1)S(1)} %slice_dynamic-update-slice_fusion.refs_0_), channel_id=1, source_target_pairs={{0,3},{1,0},{2,1},{3,2},{4,7},{5,4},{6,5},{7,6},{8,11},{9,8},{10,9... | collective-permute-start | bytes 1081352 | tf_op jit(solution)/shard_map/ppermute | solution.py:202

commit v4 on v3

--- a/solution.py
+++ b/solution.py
@@ -128,9 +128,9 @@
         for h in range(2):
             cols = pl.ds((2 * k + h) * GROUP, GROUP)
             w_value = values_ref[2 * k + h]
-            high, low = split(acc_ref[:, cols])
-            part = jnp.dot(w_value, high, preferred_element_type=f32)
-            part = part + jnp.dot(w_value, low, preferred_element_type=f32)
+            halves = jnp.concatenate(split(acc_ref[:, cols]), axis=1)
+            part = jnp.dot(w_value, halves, preferred_element_type=f32)
+            part = part[:, :GROUP] + part[:, GROUP:]
             out_ref[owner, h * VDIM : (h + 1) * VDIM] = part.astype(bf16)
             stats += thirds(m_ref[:, cols]) + thirds(l_ref[:, cols])
         stats.append(jnp.zeros((4, GROUP), bf16))
@@ -207,9 +207,8 @@
     )
     qcat, values = call(query_kernel, shapes, *qws)
     zs = ZH * ZL
-    up = [((z, 1), ((z + 1) % zs, 1)) for z in range(zs)]
-    down = [((z, 0), ((z - 1) % zs, 0)) for z in range(zs)]
-    pairs = [(z * CS + c, to_z * CS + to_c) for (z, c), (to_z, to_c) in up + down]
+    pairs = [(z * CS, (z ^ 1) * CS) for z in range(zs)]
+    pairs += [(z * CS + 1, ((z + 1 if z % 2 else z - 1) % zs) * CS + 1) for z in range(zs)]
     far = lax.ppermute(near, ("zh", "zl", "c"), pairs)
     swap = [(0, 1), (1, 0)]
     near_other = lax.ppermute(near, "c", swap)

time: 100 us -> 100 us (level)
  no operation moved by 1% of the time
where the time goes in v4:
time: 100 us; the launch traced here: 99.7 us
  waiting for transfers between devices  39.6 us (40%)
  starting transfers between devices  34.1 us (34%)
  Pallas kernels  13.9 us (14%)
  blocking collectives  10.9 us (11%)
  local copies, waits for them, and re-layouts  1 us (1%)
    all_to_all x1, waiting for transfers between devices, steps(): lax.all_to_all(copies, ('y', 'zh'), split_axis=0, concat_axis=0, tiled=True)  19.6 us
    all_to_all x1, starting transfers between devices, steps(): lax.all_to_all(copies, ('y', 'zh'), split_axis=0, concat_axis=0, tiled=True)  15.7 us
    pallas_call x7, Pallas kernels, call(): pl.pallas_call(kernel, out_shape=out_shape, in_specs=[pl.BlockSpec(memory...  13.9 us
    ppermute x3, waiting for transfers between devices, steps(): lax.ppermute(own, 'x', [(i, (i + k) % XS) for i in range(XS)])  12.8 us
    ppermute x3, starting transfers between devices, steps(): lax.ppermute(own, 'x', [(i, (i + k) % XS) for i in range(XS)])  11.4 us
    all_to_all x1, blocking collectives, steps(): parts = lax.all_to_all(parts, 'x', split_axis=0, concat_axis=0, tiled=True)  10.9 us
    ppermute x1, waiting for transfers between devices, steps(): far = lax.ppermute(near, ('zh', 'zl', 'c'), pairs)  7.16 us
    ppermute x1, starting transfers between devices, steps(): far = lax.ppermute(near, ('zh', 'zl', 'c'), pairs)  3.13 us
  transfers between devices with their start and end apart: 7, of which 5 were waited for; matrix products, arithmetic and copies ran while one was open for 0% of the time, Pallas kernels for 9%

profile of v4, /device:TPU:40, one launch (start us, length us, event | category | flops | bytes accessed | tf_op | source)
XLA Modules:
  0.0 99.7 jit_solution(4972758585441233271)
XLA Ops:
  0.0 0.7 copy-done
  0.7 0.9 shard_map.38
  1.7 15.7 %all-to-all-start = ((bf16[32,80,128]{2,1,0:T(8,128)(2,1)}), bf16[32,80,128]{2,1,0:T(8,128)(2,1)S(1)}, u32[]{:S(2)}, u32[]{:S(2)}) async-start(bf16[32,80,128]{2,1,0:T(8,128)(2,1)} %shard_map.38), calls=%async_computation | async-start | bytes 1310720 | tf_op jit(solution)/shard_map/all_to_all | solution.py:193
  17.4 0.1 fusion
  17.5 19.6 %all-to-all-done.kv_ref = bf16[32,80,128]{2,1,0:T(8,128)(2,1)S(1)} async-done(((bf16[32,80,128]{2,1,0:T(8,128)(2,1)}), bf16[32,80,128]{2,1,0:T(8,128)(2,1)S(1)}, u32[]{:S(2)}, u32[]{:S(2)}) %all-to-all-start) | async-done | bytes 655392 | tf_op jit(solution)/shard_map/all_to_all | solution.py:193
  37.1 3.1 %collective-permute-start.3 = (bf16[32,80,128]{2,1,0:T(8,128)(2,1)S(1)}, bf16[32,80,128]{2,1,0:T(8,128)(2,1)S(1)}, u32[]{:S(2)}, u32[]{:S(2)}) collective-permute-start(bf16[32,80,128]{2,1,0:T(8,128)(2,1)S(1)} %all-to-all-done.kv_ref), channel_id=1, source_target_pairs={{0,8},{8,0},{16,24},{24,16},{32,40},{40,32},{48,56},{56,48},{4,60}... | collective-permute-start | bytes 1966088 | tf_op jit(solution)/shard_map/ppermute | solution.py:212
  40.3 0.1 slice_dynamic-update-slice_fusion.4
  40.4 0.1 maximum_dynamic-update-slice_fusion
  40.5 1.9 %collective-permute-start.5 = (bf16[32,80,128]{2,1,0:T(8,128)(2,1)S(1)}, bf16[32,80,128]{2,1,0:T(8,128)(2,1)S(1)}, u32[]{:S(2)}, u32[]{:S(2)}) collective-permute-start(bf16[32,80,128]{2,1,0:T(8,128)(2,1)S(1)} %all-to-all-done.kv_ref), channel_id=1, source_target_pairs={{0,4},{4,0},{1,5},{5,1},{2,6},{6,2},{3,7},{7,3},{8,12},{12,8},{9,1... | collective-permute-start | bytes 1966088 | tf_op jit(solution)/shard_map/ppermute | solution.py:214
  42.5 7.2 %collective-permute-done.3.kv_ref = bf16[32,80,128]{2,1,0:T(8,128)(2,1)S(1)} collective-permute-done((bf16[32,80,128]{2,1,0:T(8,128)(2,1)S(1)}, bf16[32,80,128]{2,1,0:T(8,128)(2,1)S(1)}, u32[]{:S(2)}, u32[]{:S(2)}) %collective-permute-start.3) | collective-permute-done | bytes 655392 | tf_op jit(solution)/shard_map/ppermute | solution.py:212
  49.6 1.9 %collective-permute-start.4 = (bf16[32,80,128]{2,1,0:T(8,128)(2,1)S(1)}, bf16[32,80,128]{2,1,0:T(8,128)(2,1)S(1)}, u32[]{:S(2)}, u32[]{:S(2)}) collective-permute-start(bf16[32,80,128]{2,1,0:T(8,128)(2,1)S(1)} %collective-permute-done.3.kv_ref), channel_id=1, source_target_pairs={{0,4},{4,0},{1,5},{5,1},{2,6},{6,2},{3,7},{7,3},{8,12},{12,8},{9,1... | collective-permute-start | bytes 1966088 | tf_op jit(solution)/shard_map/ppermute | solution.py:217
  51.6 3.4 %collective-permute-start = (bf16[1408,128]{1,0:T(8,128)(2,1)S(1)}, bf16[1408,128]{1,0:T(8,128)(2,1)S(1)}, u32[]{:S(2)}, u32[]{:S(2)}) collective-permute-start(bf16[1408,128]{1,0:T(8,128)(2,1)S(1)} %slice_dynamic-update-slice_fusion.refs_0_), channel_id=1, source_target_pairs={{0,1},{1,2},{2,3},{3,0},{4,5},{5,6},{6,7},{7,4},{8,9},{9,10},{10,1... | collective-permute-start | bytes 1081352 | tf_op jit(solution)/shard_map/ppermute | solution.py:202
  55.0 4.6 %collective-permute-start.1 = (bf16[1408,128]{1,0:T(8,128)(2,1)S(1)}, bf16[1408,128]{1,0:T(8,128)(2,1)S(1)}, u32[]{:S(2)}, u32[]{:S(2)}) collective-permute-start(bf16[1408,128]{1,0:T(8,128)(2,1)S(1)} %slice_dynamic-update-slice_fusion.refs_0_), channel_id=1, source_target_pairs={{0,2},{1,3},{2,0},{3,1},{4,6},{5,7},{6,4},{7,5},{8,10},{9,11},{10,... | collective-permute-start | bytes 1081352 | tf_op jit(solution)/shard_map/ppermute | solution.py:202
  59.6 3.3 %collective-permute-start.2 = (bf16[1408,128]{1,0:T(8,128)(2,1)S(1)}, bf16[1408,128]{1,0:T(8,128)(2,1)S(1)}, u32[]{:S(2)}, u32[]{:S(2)}) collective-permute-start(bf16[1408,128]{1,0:T(8,128)(2,1)S(1)} %slice_dynamic-update-slice_fusion.refs_0_), channel_id=1, source_target_pairs={{0,3},{1,0},{2,1},{3,2},{4,7},{5,4},{6,5},{7,6},{8,11},{9,8},{10,9... | collective-permute-start | bytes 1081352 | tf_op jit(solution)/shard_map/ppermute | solution.py:202
  63.0 2.5 %collective-permute-done.refs_1_ = bf16[1408,128]{1,0:T(8,128)(2,1)S(1)} collective-permute-done((bf16[1408,128]{1,0:T(8,128)(2,1)S(1)}, bf16[1408,128]{1,0:T(8,128)(2,1)S(1)}, u32[]{:S(2)}, u32[]{:S(2)}) %collective-permute-start) | collective-permute-done | bytes 360480 | tf_op jit(solution)/shard_map/ppermute | solution.py:202
  65.5 8.7 %collective-permute-done.1.refs_2_ = bf16[1408,128]{1,0:T(8,128)(2,1)S(1)} collective-permute-done((bf16[1408,128]{1,0:T(8,128)(2,1)S(1)}, bf16[1408,128]{1,0:T(8,128)(2,1)S(1)}, u32[]{:S(2)}, u32[]{:S(2)}) %collective-permute-start.1) | collective-permute-done | bytes 360480 | tf_op jit(solution)/shard_map/ppermute | solution.py:202
  74.2 1.6 %collective-permute-done.2.refs_3_ = bf16[1408,128]{1,0:T(8,128)(2,1)S(1)} collective-permute-done((bf16[1408,128]{1,0:T(8,128)(2,1)S(1)}, bf16[1408,128]{1,0:T(8,128)(2,1)S(1)}, u32[]{:S(2)}, u32[]{:S(2)}) %collective-permute-start.2) | collective-permute-done | bytes 360480 | tf_op jit(solution)/shard_map/ppermute | solution.py:202
  75.8 0.4 shard_map.37
  76.2 2.8 %shard_map.39 = (f32[1,1024]{1,0:T(1,128)S(1)}, f32[1,1024]{1,0:T(1,128)S(1)}, f32[256,1024]{1,0:T(8,128)S(1)}) custom-call(bf16[32,80,128]{2,1,0:T(8,128)(2,1)S(1)} %all-to-all-done.kv_ref, bf16[768,1024]{1,0:T(8,128)(2,1)S(1)} %get-tuple-element.17.qcat_ref), custom_call_target="tpu_custom_call" | custom-call | tf_op jit(solution)/shard_map/pallas_call | solution.py:159
  79.0 2.8 %shard_map.40 = (f32[1,1024]{1,0:T(1,128)S(1)}, f32[1,1024]{1,0:T(1,128)S(1)}, f32[256,1024]{1,0:T(8,128)S(1)}) custom-call(bf16[32,80,128]{2,1,0:T(8,128)(2,1)S(1)} %collective-permute-done.5.kv_ref, bf16[768,1024]{1,0:T(8,128)(2,1)S(1)} %get-tuple-element.17.qcat_ref, f32[1,1024]{1,0:T(1,128)S(1)} %get-tuple-element.18.m_in, ...), custom_call_target="tpu_custom_call" | custom-call | tf_op jit(solution)/shard_map/pallas_call | solution.py:159
  81.8 2.8 %shard_map.41 = (f32[1,1024]{1,0:T(1,128)S(1)}, f32[1,1024]{1,0:T(1,128)S(1)}, f32[256,1024]{1,0:T(8,128)S(1)}) custom-call(bf16[32,80,128]{2,1,0:T(8,128)(2,1)S(1)} %collective-permute-done.3.kv_ref, bf16[768,1024]{1,0:T(8,128)(2,1)S(1)} %get-tuple-element.17.qcat_ref, f32[1,1024]{1,0:T(1,128)S(1)} %get-tuple-element.21.m_in, ...), custom_call_target="tpu_custom_call" | custom-call | tf_op jit(solution)/shard_map/pallas_call | solution.py:159
  84.7 3.3 %shard_map.42 = bf16[4,272,128]{2,1,0:T(8,128)(2,1)S(1)} custom-call(bf16[8,128,256]{2,1,0:T(8,128)(2,1)S(1)} %get-tuple-element.16.values_ref, bf16[32,80,128]{2,1,0:T(8,128)(2,1)S(1)} %collective-permute-done.4.kv_ref, bf16[768,1024]{1,0:T(8,128)(2,1)S(1)} %get-tuple-element.17.qcat_ref, f32[1,1024]{1,0:T(1,128)S(1)} %get-tuple-element.24.m_in, ...), custom_call_target="tpu_custom_call" | custom-call | tf_op jit(solution)/shard_map/pallas_call | solution.py:159
  88.0 10.9 %all_to_all.10.parts_ref = bf16[4,272,128]{2,1,0:T(8,128)(2,1)S(1)} all-to-all(bf16[4,272,128]{2,1,0:T(8,128)(2,1)S(1)} %shard_map.42), channel_id=1, replica_groups=mesh['y'=8,'zh'=4,'zl'=2,'c'=2,'x'=4] {'x'}, dimensions={0} | all-to-all | bytes 557056 | tf_op jit(solution)/shard_map/all_to_all | solution.py:225
  98.9 0.8 shard_map.43
  (12 shorter events, 0.1 us)
Async XLA Ops:
  0.0 0.7 copy-start
  0.7 16.7 %copy-start.2 = (bf16[128,384]{1,0:T(8,128)(2,1)S(1)}, bf16[128,384]{1,0:T(8,128)(2,1)}, u32[]{:S(2)}) copy-start(bf16[128,384]{1,0:T(8,128)(2,1)} %param.3) | copy-start | bytes 294916
  0.7 39.7 %copy-start.1 = (bf16[256,512]{1,0:T(8,128)(2,1)S(1)}, bf16[256,512]{1,0:T(8,128)(2,1)}, u32[]{:S(2)}) copy-start(bf16[256,512]{1,0:T(8,128)(2,1)} %param.5) | copy-start | bytes 786436
  1.7 35.5 %all-to-all-start = ((bf16[32,80,128]{2,1,0:T(8,128)(2,1)}), bf16[32,80,128]{2,1,0:T(8,128)(2,1)S(1)}, u32[]{:S(2)}, u32[]{:S(2)}) async-start(bf16[32,80,128]{2,1,0:T(8,128)(2,1)} %shard_map.38), calls=%async_computation | async-start | bytes 1310720 | tf_op jit(solution)/shard_map/all_to_all | solution.py:193
  37.1 12.5 %collective-permute-start.3 = (bf16[32,80,128]{2,1,0:T(8,128)(2,1)S(1)}, bf16[32,80,128]{2,1,0:T(8,128)(2,1)S(1)}, u32[]{:S(2)}, u32[]{:S(2)}) collective-permute-start(bf16[32,80,128]{2,1,0:T(8,128)(2,1)S(1)} %all-to-all-done.kv_ref), channel_id=1, source_target_pairs={{0,8},{8,0},{16,24},{24,16},{32,40},{40,32},{48,56},{56,48},{4,60}... | collective-permute-start | bytes 1966088 | tf_op jit(solution)/shard_map/ppermute | solution.py:212
  40.5 38.5 %collective-permute-start.5 = (bf16[32,80,128]{2,1,0:T(8,128)(2,1)S(1)}, bf16[32,80,128]{2,1,0:T(8,128)(2,1)S(1)}, u32[]{:S(2)}, u32[]{:S(2)}) collective-permute-start(bf16[32,80,128]{2,1,0:T(8,128)(2,1)S(1)} %all-to-all-done.kv_ref), channel_id=1, source_target_pairs={{0,4},{4,0},{1,5},{5,1},{2,6},{6,2},{3,7},{7,3},{8,12},{12,8},{9,1... | collective-permute-start | bytes 1966088 | tf_op jit(solution)/shard_map/ppermute | solution.py:214
  49.6 35.1 %collective-permute-start.4 = (bf16[32,80,128]{2,1,0:T(8,128)(2,1)S(1)}, bf16[32,80,128]{2,1,0:T(8,128)(2,1)S(1)}, u32[]{:S(2)}, u32[]{:S(2)}) collective-permute-start(bf16[32,80,128]{2,1,0:T(8,128)(2,1)S(1)} %collective-permute-done.3.kv_ref), channel_id=1, source_target_pairs={{0,4},{4,0},{1,5},{5,1},{2,6},{6,2},{3,7},{7,3},{8,12},{12,8},{9,1... | collective-permute-start | bytes 1966088 | tf_op jit(solution)/shard_map/ppermute | solution.py:217
  51.6 13.9 %collective-permute-start = (bf16[1408,128]{1,0:T(8,128)(2,1)S(1)}, bf16[1408,128]{1,0:T(8,128)(2,1)S(1)}, u32[]{:S(2)}, u32[]{:S(2)}) collective-permute-start(bf16[1408,128]{1,0:T(8,128)(2,1)S(1)} %slice_dynamic-update-slice_fusion.refs_0_), channel_id=1, source_target_pairs={{0,1},{1,2},{2,3},{3,0},{4,5},{5,6},{6,7},{7,4},{8,9},{9,10},{10,1... | collective-permute-start | bytes 1081352 | tf_op jit(solution)/shard_map/ppermute | solution.py:202
  55.0 19.2 %collective-permute-start.1 = (bf16[1408,128]{1,0:T(8,128)(2,1)S(1)}, bf16[1408,128]{1,0:T(8,128)(2,1)S(1)}, u32[]{:S(2)}, u32[]{:S(2)}) collective-permute-start(bf16[1408,128]{1,0:T(8,128)(2,1)S(1)} %slice_dynamic-update-slice_fusion.refs_0_), channel_id=1, source_target_pairs={{0,2},{1,3},{2,0},{3,1},{4,6},{5,7},{6,4},{7,5},{8,10},{9,11},{10,... | collective-permute-start | bytes 1081352 | tf_op jit(solution)/shard_map/ppermute | solution.py:202
  59.6 16.1 %collective-permute-start.2 = (bf16[1408,128]{1,0:T(8,128)(2,1)S(1)}, bf16[1408,128]{1,0:T(8,128)(2,1)S(1)}, u32[]{:S(2)}, u32[]{:S(2)}) collective-permute-start(bf16[1408,128]{1,0:T(8,128)(2,1)S(1)} %slice_dynamic-update-slice_fusion.refs_0_), channel_id=1, source_target_pairs={{0,3},{1,0},{2,1},{3,2},{4,7},{5,4},{6,5},{7,6},{8,11},{9,8},{10,9... | collective-permute-start | bytes 1081352 | tf_op jit(solution)/shard_map/ppermute | solution.py:202

commit v5 on v4

--- a/solution.py
+++ b/solution.py
@@ -57,7 +57,7 @@
 
 def attend_groups(groups, kv_ref, key_zl, key_c, qcat_ref, old, new):
     y, zh, zl, c, x = (lax.axis_index(a) for a in ("y", "zh", "zl", "c", "x"))
-    count, free = groups * KEYS, (groups - HALF) * KEYS
+    count, free = groups * KEYS, max(groups - HALF, 0) * KEYS
     block = kv_ref[0:groups]
     latent = jnp.concatenate(
         [block[:, 0:KEYS].reshape(count, 128), block[:, KEYS : 2 * KEYS].reshape(count, 128)], axis=1
@@ -94,15 +94,19 @@
     zl, c = lax.axis_index("zl"), lax.axis_index("c")
     key_zl = zl if same_parity else 1 - zl
     key_c = c if same_core else 1 - c
-    upper = lax.axis_index("y") >= YS // 2
-
-    @pl.when(upper)
+    y = lax.axis_index("y")
+
+    @pl.when(y >= YS // 2)
     def _():
         attend_groups(2 * HALF, kv_ref, key_zl, key_c, qcat_ref, old, new)
 
-    @pl.when(jnp.logical_not(upper))
+    @pl.when((y >= YS // 4) & (y < YS // 2))
     def _():
         attend_groups(HALF, kv_ref, key_zl, key_c, qcat_ref, old, new)
+
+    @pl.when(y < YS // 4)
+    def _():
+        attend_groups(HALF // 2, kv_ref, key_zl, key_c, qcat_ref, old, new)
 
 
 def attend_first(kv_ref, qcat_ref, m_ref, l_ref, acc_ref):

time: 100 us -> 100 us (level)
  no operation moved by 1% of the time
where the time goes in v5:
time: 100 us; the launch traced here: 99.7 us
  waiting for transfers between devices  39.6 us (40%)
  starting transfers between devices  34.1 us (34%)
  Pallas kernels  13.9 us (14%)
  blocking collectives  10.9 us (11%)
  local copies, waits for them, and re-layouts  1 us (1%)
    all_to_all x1, waiting for transfers between devices, steps(): lax.all_to_all(copies, ('y', 'zh'), split_axis=0, concat_axis=0, tiled=True)  19.6 us
    all_to_all x1, starting transfers between devices, steps(): lax.all_to_all(copies, ('y', 'zh'), split_axis=0, concat_axis=0, tiled=True)  15.7 us
    pallas_call x7, Pallas kernels, call(): pl.pallas_call(kernel, out_shape=out_shape, in_specs=[pl.BlockSpec(memory...  13.9 us
    ppermute x3, waiting for transfers between devices, steps(): lax.ppermute(own, 'x', [(i, (i + k) % XS) for i in range(XS)])  12.8 us
    ppermute x3, starting transfers between devices, steps(): lax.ppermute(own, 'x', [(i, (i + k) % XS) for i in range(XS)])  11.4 us
    all_to_all x1, blocking collectives, steps(): parts = lax.all_to_all(parts, 'x', split_axis=0, concat_axis=0, tiled=True)  10.9 us
    ppermute x1, waiting for transfers between devices, steps(): far = lax.ppermute(near, ('zh', 'zl', 'c'), pairs)  7.16 us
    ppermute x1, starting transfers between devices, steps(): far = lax.ppermute(near, ('zh', 'zl', 'c'), pairs)  3.13 us
  transfers between devices with their start and end apart: 7, of which 5 were waited for; matrix products, arithmetic and copies ran while one was open for 0% of the time, Pallas kernels for 9%

profile of v5, /device:TPU:40, one launch (start us, length us, event | category | flops | bytes accessed | tf_op | source)
XLA Modules:
  0.0 99.7 jit_solution(1236336219480963502)
XLA Ops:
  0.0 0.7 copy-done
  0.7 0.9 shard_map.38
  1.7 15.7 %all-to-all-start = ((bf16[32,80,128]{2,1,0:T(8,128)(2,1)}), bf16[32,80,128]{2,1,0:T(8,128)(2,1)S(1)}, u32[]{:S(2)}, u32[]{:S(2)}) async-start(bf16[32,80,128]{2,1,0:T(8,128)(2,1)} %shard_map.38), calls=%async_computation | async-start | bytes 1310720 | tf_op jit(solution)/shard_map/all_to_all | solution.py:197
  17.4 0.1 fusion
  17.5 19.6 %all-to-all-done.kv_ref = bf16[32,80,128]{2,1,0:T(8,128)(2,1)S(1)} async-done(((bf16[32,80,128]{2,1,0:T(8,128)(2,1)}), bf16[32,80,128]{2,1,0:T(8,128)(2,1)S(1)}, u32[]{:S(2)}, u32[]{:S(2)}) %all-to-all-start) | async-done | bytes 655392 | tf_op jit(solution)/shard_map/all_to_all | solution.py:197
  37.1 3.1 %collective-permute-start.3 = (bf16[32,80,128]{2,1,0:T(8,128)(2,1)S(1)}, bf16[32,80,128]{2,1,0:T(8,128)(2,1)S(1)}, u32[]{:S(2)}, u32[]{:S(2)}) collective-permute-start(bf16[32,80,128]{2,1,0:T(8,128)(2,1)S(1)} %all-to-all-done.kv_ref), channel_id=1, source_target_pairs={{0,8},{8,0},{16,24},{24,16},{32,40},{40,32},{48,56},{56,48},{4,60}... | collective-permute-start | bytes 1966088 | tf_op jit(solution)/shard_map/ppermute | solution.py:216
  40.3 0.1 slice_dynamic-update-slice_fusion.4
  40.4 0.1 maximum_dynamic-update-slice_fusion
  40.5 1.9 %collective-permute-start.5 = (bf16[32,80,128]{2,1,0:T(8,128)(2,1)S(1)}, bf16[32,80,128]{2,1,0:T(8,128)(2,1)S(1)}, u32[]{:S(2)}, u32[]{:S(2)}) collective-permute-start(bf16[32,80,128]{2,1,0:T(8,128)(2,1)S(1)} %all-to-all-done.kv_ref), channel_id=1, source_target_pairs={{0,4},{4,0},{1,5},{5,1},{2,6},{6,2},{3,7},{7,3},{8,12},{12,8},{9,1... | collective-permute-start | bytes 1966088 | tf_op jit(solution)/shard_map/ppermute | solution.py:218
  42.5 7.2 %collective-permute-done.3.kv_ref = bf16[32,80,128]{2,1,0:T(8,128)(2,1)S(1)} collective-permute-done((bf16[32,80,128]{2,1,0:T(8,128)(2,1)S(1)}, bf16[32,80,128]{2,1,0:T(8,128)(2,1)S(1)}, u32[]{:S(2)}, u32[]{:S(2)}) %collective-permute-start.3) | collective-permute-done | bytes 655392 | tf_op jit(solution)/shard_map/ppermute | solution.py:216
  49.6 1.9 %collective-permute-start.4 = (bf16[32,80,128]{2,1,0:T(8,128)(2,1)S(1)}, bf16[32,80,128]{2,1,0:T(8,128)(2,1)S(1)}, u32[]{:S(2)}, u32[]{:S(2)}) collective-permute-start(bf16[32,80,128]{2,1,0:T(8,128)(2,1)S(1)} %collective-permute-done.3.kv_ref), channel_id=1, source_target_pairs={{0,4},{4,0},{1,5},{5,1},{2,6},{6,2},{3,7},{7,3},{8,12},{12,8},{9,1... | collective-permute-start | bytes 1966088 | tf_op jit(solution)/shard_map/ppermute | solution.py:221
  51.6 3.4 %collective-permute-start = (bf16[1408,128]{1,0:T(8,128)(2,1)S(1)}, bf16[1408,128]{1,0:T(8,128)(2,1)S(1)}, u32[]{:S(2)}, u32[]{:S(2)}) collective-permute-start(bf16[1408,128]{1,0:T(8,128)(2,1)S(1)} %slice_dynamic-update-slice_fusion.refs_0_), channel_id=1, source_target_pairs={{0,1},{1,2},{2,3},{3,0},{4,5},{5,6},{6,7},{7,4},{8,9},{9,10},{10,1... | collective-permute-start | bytes 1081352 | tf_op jit(solution)/shard_map/ppermute | solution.py:206
  55.0 4.6 %collective-permute-start.1 = (bf16[1408,128]{1,0:T(8,128)(2,1)S(1)}, bf16[1408,128]{1,0:T(8,128)(2,1)S(1)}, u32[]{:S(2)}, u32[]{:S(2)}) collective-permute-start(bf16[1408,128]{1,0:T(8,128)(2,1)S(1)} %slice_dynamic-update-slice_fusion.refs_0_), channel_id=1, source_target_pairs={{0,2},{1,3},{2,0},{3,1},{4,6},{5,7},{6,4},{7,5},{8,10},{9,11},{10,... | collective-permute-start | bytes 1081352 | tf_op jit(solution)/shard_map/ppermute | solution.py:206
  59.6 3.3 %collective-permute-start.2 = (bf16[1408,128]{1,0:T(8,128)(2,1)S(1)}, bf16[1408,128]{1,0:T(8,128)(2,1)S(1)}, u32[]{:S(2)}, u32[]{:S(2)}) collective-permute-start(bf16[1408,128]{1,0:T(8,128)(2,1)S(1)} %slice_dynamic-update-slice_fusion.refs_0_), channel_id=1, source_target_pairs={{0,3},{1,0},{2,1},{3,2},{4,7},{5,4},{6,5},{7,6},{8,11},{9,8},{10,9... | collective-permute-start | bytes 1081352 | tf_op jit(solution)/shard_map/ppermute | solution.py:206
  63.0 2.5 %collective-permute-done.refs_1_ = bf16[1408,128]{1,0:T(8,128)(2,1)S(1)} collective-permute-done((bf16[1408,128]{1,0:T(8,128)(2,1)S(1)}, bf16[1408,128]{1,0:T(8,128)(2,1)S(1)}, u32[]{:S(2)}, u32[]{:S(2)}) %collective-permute-start) | collective-permute-done | bytes 360480 | tf_op jit(solution)/shard_map/ppermute | solution.py:206
  65.5 8.7 %collective-permute-done.1.refs_2_ = bf16[1408,128]{1,0:T(8,128)(2,1)S(1)} collective-permute-done((bf16[1408,128]{1,0:T(8,128)(2,1)S(1)}, bf16[1408,128]{1,0:T(8,128)(2,1)S(1)}, u32[]{:S(2)}, u32[]{:S(2)}) %collective-permute-start.1) | collective-permute-done | bytes 360480 | tf_op jit(solution)/shard_map/ppermute | solution.py:206
  74.2 1.6 %collective-permute-done.2.refs_3_ = bf16[1408,128]{1,0:T(8,128)(2,1)S(1)} collective-permute-done((bf16[1408,128]{1,0:T(8,128)(2,1)S(1)}, bf16[1408,128]{1,0:T(8,128)(2,1)S(1)}, u32[]{:S(2)}, u32[]{:S(2)}) %collective-permute-start.2) | collective-permute-done | bytes 360480 | tf_op jit(solution)/shard_map/ppermute | solution.py:206
  75.8 0.4 shard_map.37
  76.2 2.8 %shard_map.39 = (f32[1,1024]{1,0:T(1,128)S(1)}, f32[1,1024]{1,0:T(1,128)S(1)}, f32[256,1024]{1,0:T(8,128)S(1)}) custom-call(bf16[32,80,128]{2,1,0:T(8,128)(2,1)S(1)} %all-to-all-done.kv_ref, bf16[768,1024]{1,0:T(8,128)(2,1)S(1)} %get-tuple-element.17.qcat_ref), custom_call_target="tpu_custom_call" | custom-call | tf_op jit(solution)/shard_map/pallas_call | solution.py:163
  79.0 2.8 %shard_map.40 = (f32[1,1024]{1,0:T(1,128)S(1)}, f32[1,1024]{1,0:T(1,128)S(1)}, f32[256,1024]{1,0:T(8,128)S(1)}) custom-call(bf16[32,80,128]{2,1,0:T(8,128)(2,1)S(1)} %collective-permute-done.5.kv_ref, bf16[768,1024]{1,0:T(8,128)(2,1)S(1)} %get-tuple-element.17.qcat_ref, f32[1,1024]{1,0:T(1,128)S(1)} %get-tuple-element.18.m_in, ...), custom_call_target="tpu_custom_call" | custom-call | tf_op jit(solution)/shard_map/pallas_call | solution.py:163
  81.8 3.0 %shard_map.41 = (f32[1,1024]{1,0:T(1,128)S(1)}, f32[1,1024]{1,0:T(1,128)S(1)}, f32[256,1024]{1,0:T(8,128)S(1)}) custom-call(bf16[32,80,128]{2,1,0:T(8,128)(2,1)S(1)} %collective-permute-done.3.kv_ref, bf16[768,1024]{1,0:T(8,128)(2,1)S(1)} %get-tuple-element.17.qcat_ref, f32[1,1024]{1,0:T(1,128)S(1)} %get-tuple-element.21.m_in, ...), custom_call_target="tpu_custom_call" | custom-call | tf_op jit(solution)/shard_map/pallas_call | solution.py:163
  84.9 3.2 %shard_map.42 = bf16[4,272,128]{2,1,0:T(8,128)(2,1)S(1)} custom-call(bf16[8,128,256]{2,1,0:T(8,128)(2,1)S(1)} %get-tuple-element.16.values_ref, bf16[32,80,128]{2,1,0:T(8,128)(2,1)S(1)} %collective-permute-done.4.kv_ref, bf16[768,1024]{1,0:T(8,128)(2,1)S(1)} %get-tuple-element.17.qcat_ref, f32[1,1024]{1,0:T(1,128)S(1)} %get-tuple-element.24.m_in, ...), custom_call_target="tpu_custom_call" | custom-call | tf_op jit(solution)/shard_map/pallas_call | solution.py:163
  88.1 10.9 %all_to_all.10.parts_ref = bf16[4,272,128]{2,1,0:T(8,128)(2,1)S(1)} all-to-all(bf16[4,272,128]{2,1,0:T(8,128)(2,1)S(1)} %shard_map.42), channel_id=1, replica_groups=mesh['y'=8,'zh'=4,'zl'=2,'c'=2,'x'=4] {'x'}, dimensions={0} | all-to-all | bytes 557056 | tf_op jit(solution)/shard_map/all_to_all | solution.py:229
  98.9 0.8 shard_map.43
  (12 shorter events, 0.1 us)
Async XLA Ops:
  0.0 0.7 copy-start
  0.7 16.7 %copy-start.2 = (bf16[128,384]{1,0:T(8,128)(2,1)S(1)}, bf16[128,384]{1,0:T(8,128)(2,1)}, u32[]{:S(2)}) copy-start(bf16[128,384]{1,0:T(8,128)(2,1)} %param.3) | copy-start | bytes 294916
  0.7 39.7 %copy-start.1 = (bf16[256,512]{1,0:T(8,128)(2,1)S(1)}, bf16[256,512]{1,0:T(8,128)(2,1)}, u32[]{:S(2)}) copy-start(bf16[256,512]{1,0:T(8,128)(2,1)} %param.5) | copy-start | bytes 786436
  1.7 35.5 %all-to-all-start = ((bf16[32,80,128]{2,1,0:T(8,128)(2,1)}), bf16[32,80,128]{2,1,0:T(8,128)(2,1)S(1)}, u32[]{:S(2)}, u32[]{:S(2)}) async-start(bf16[32,80,128]{2,1,0:T(8,128)(2,1)} %shard_map.38), calls=%async_computation | async-start | bytes 1310720 | tf_op jit(solution)/shard_map/all_to_all | solution.py:197
  37.1 12.5 %collective-permute-start.3 = (bf16[32,80,128]{2,1,0:T(8,128)(2,1)S(1)}, bf16[32,80,128]{2,1,0:T(8,128)(2,1)S(1)}, u32[]{:S(2)}, u32[]{:S(2)}) collective-permute-start(bf16[32,80,128]{2,1,0:T(8,128)(2,1)S(1)} %all-to-all-done.kv_ref), channel_id=1, source_target_pairs={{0,8},{8,0},{16,24},{24,16},{32,40},{40,32},{48,56},{56,48},{4,60}... | collective-permute-start | bytes 1966088 | tf_op jit(solution)/shard_map/ppermute | solution.py:216
  40.5 38.5 %collective-permute-start.5 = (bf16[32,80,128]{2,1,0:T(8,128)(2,1)S(1)}, bf16[32,80,128]{2,1,0:T(8,128)(2,1)S(1)}, u32[]{:S(2)}, u32[]{:S(2)}) collective-permute-start(bf16[32,80,128]{2,1,0:T(8,128)(2,1)S(1)} %all-to-all-done.kv_ref), channel_id=1, source_target_pairs={{0,4},{4,0},{1,5},{5,1},{2,6},{6,2},{3,7},{7,3},{8,12},{12,8},{9,1... | collective-permute-start | bytes 1966088 | tf_op jit(solution)/shard_map/ppermute | solution.py:218
  49.6 35.3 %collective-permute-start.4 = (bf16[32,80,128]{2,1,0:T(8,128)(2,1)S(1)}, bf16[32,80,128]{2,1,0:T(8,128)(2,1)S(1)}, u32[]{:S(2)}, u32[]{:S(2)}) collective-permute-start(bf16[32,80,128]{2,1,0:T(8,128)(2,1)S(1)} %collective-permute-done.3.kv_ref), channel_id=1, source_target_pairs={{0,4},{4,0},{1,5},{5,1},{2,6},{6,2},{3,7},{7,3},{8,12},{12,8},{9,1... | collective-permute-start | bytes 1966088 | tf_op jit(solution)/shard_map/ppermute | solution.py:221
  51.6 13.9 %collective-permute-start = (bf16[1408,128]{1,0:T(8,128)(2,1)S(1)}, bf16[1408,128]{1,0:T(8,128)(2,1)S(1)}, u32[]{:S(2)}, u32[]{:S(2)}) collective-permute-start(bf16[1408,128]{1,0:T(8,128)(2,1)S(1)} %slice_dynamic-update-slice_fusion.refs_0_), channel_id=1, source_target_pairs={{0,1},{1,2},{2,3},{3,0},{4,5},{5,6},{6,7},{7,4},{8,9},{9,10},{10,1... | collective-permute-start | bytes 1081352 | tf_op jit(solution)/shard_map/ppermute | solution.py:206
  55.0 19.2 %collective-permute-start.1 = (bf16[1408,128]{1,0:T(8,128)(2,1)S(1)}, bf16[1408,128]{1,0:T(8,128)(2,1)S(1)}, u32[]{:S(2)}, u32[]{:S(2)}) collective-permute-start(bf16[1408,128]{1,0:T(8,128)(2,1)S(1)} %slice_dynamic-update-slice_fusion.refs_0_), channel_id=1, source_target_pairs={{0,2},{1,3},{2,0},{3,1},{4,6},{5,7},{6,4},{7,5},{8,10},{9,11},{10,... | collective-permute-start | bytes 1081352 | tf_op jit(solution)/shard_map/ppermute | solution.py:206
  59.6 16.1 %collective-permute-start.2 = (bf16[1408,128]{1,0:T(8,128)(2,1)S(1)}, bf16[1408,128]{1,0:T(8,128)(2,1)S(1)}, u32[]{:S(2)}, u32[]{:S(2)}) collective-permute-start(bf16[1408,128]{1,0:T(8,128)(2,1)S(1)} %slice_dynamic-update-slice_fusion.refs_0_), channel_id=1, source_target_pairs={{0,3},{1,0},{2,1},{3,2},{4,7},{5,4},{6,5},{7,6},{8,11},{9,8},{10,9... | collective-permute-start | bytes 1081352 | tf_op jit(solution)/shard_map/ppermute | solution.py:206
